TPU v7x, 256 devices: a whole 4x4x8 slice. The times are simulated.
256 devices in a mesh: trial: 2 (over z_hi), shard: 32 (over y, x, core), cols: 4 (over z_lo).
Axes of the slice: x: 4, y: 4, z: 8 (z_hi: 2, z_lo: 4; z = z_hi * 4 + z_lo), core: 2. Of those that a mesh axis runs over, the one named last changes fastest.
Arguments:
- train_gate: bfloat16 [4096, 8192], P(('trial', 'shard'), 'cols'), parts along dimension 0, may hold values from -0.125 to 0.125
- low_gate: bfloat16 [4096, 16], P(('trial', 'shard')), parts along dimension 0, may hold values from -0.125 to 0.125
- high_gate: bfloat16 [32, 8192], P('trial', 'cols'), parts along dimension 0, may hold values from -1.5 to 1.5
- train_up: bfloat16 [4096, 8192], P(('trial', 'shard'), 'cols'), parts along dimension 0, may hold values from -0.125 to 0.125
- low_up: bfloat16 [4096, 16], P(('trial', 'shard')), parts along dimension 0, may hold values from -0.125 to 0.125
- high_up: bfloat16 [32, 8192], P('trial', 'cols'), parts along dimension 0, may hold values from -1.5 to 1.5
- norm_train: float32 [4096], P(('trial', 'shard', 'cols')), parts along dimension 0, may hold values from 0.25 to 1.75
- norm_step: float32 [4096], P(('trial', 'shard', 'cols')), parts along dimension 0, may hold values from -0.3 to 0.3
Outputs:
- serve_gate: bfloat16 [16384, 2048], P(('trial', 'cols')), parts along dimension 0
- serve_up: bfloat16 [16384, 2048], P(('trial', 'cols')), parts along dimension 0
- serve_norm: bfloat16 [4096], P('trial'), parts along dimension 0
There are 2 independent parts, one for each index of `trial`. A program takes and returns all parts, laid end to end along the dimension named above; each array names one. Nothing has to cross between parts.
All inputs are finite; a program needn't handle non-finite values.
Results may differ from a plain program's by a relative error of at most 0.001.
Values may be sent and summed in bfloat16 or wider, within the bound.
A program may use at most 128 MiB of HBM per device.

v0:
```python
import jax
import jax.numpy as jnp
from jax import lax
from jax.sharding import Mesh
from jax.sharding import PartitionSpec as P

SHARD = ("shard_0", "shard_1", "shard_2")
SHARD_COLS = ("shard_0", "shard_1", "shard_2", "cols")
TRIAL_SHARD = ("trial", "shard_0", "shard_1", "shard_2")
TRIAL_SHARD_COLS = ("trial", "shard_0", "shard_1", "shard_2", "cols")


mix_rate = 2.0


def side_by_side(arrays, axis, dim, along):
    both = jnp.concatenate(arrays, axis=along)
    result, at, finished = (lax.all_gather(both, axis, axis=dim, tiled=True), 0, [])
    for a in arrays:
        finished.append(lax.slice_in_dim(result, at, at + a.shape[along], axis=along))
        at += a.shape[along]
    return tuple(finished)


def joined_along(tiles, dim):
    tiles = jnp.moveaxis(tiles, 0, dim)
    lengths = tiles.shape
    return tiles.reshape(*lengths[:dim], lengths[dim] * lengths[dim + 1], *lengths[dim + 2 :])


def all_blocks(shard, axes, order):
    tiles = shard
    for k in order:
        tiles = lax.all_gather(tiles, axes[k])
    done = order[::-1]
    back = [done.index(k) for k in range(len(axes))]
    tiles = tiles.transpose(*back, *range(len(axes), tiles.ndim))
    return tiles.reshape(-1, *shard.shape)


def gathered_by_axis(shard, axes, order, dim):
    return joined_along(all_blocks(shard, axes, order), dim)


def local(train_gate, low_gate, high_gate, train_up, low_up, high_up, norm_train, norm_step):
    fresh_gate = train_gate.astype(jnp.float32) + mix_rate * jnp.dot(
        low_gate, high_gate, preferred_element_type=jnp.float32
    )
    fresh_up = train_up.astype(jnp.float32) + mix_rate * jnp.dot(
        low_up, high_up, preferred_element_type=jnp.float32
    )
    narrow_gate, narrow_up = (fresh_gate.astype(jnp.bfloat16), fresh_up.astype(jnp.bfloat16))
    serve_gate, serve_up = side_by_side((narrow_gate, narrow_up), SHARD, 0, 1)
    serve_gate, serve_up = (serve_gate.T, serve_up.T)
    serve_norm = gathered_by_axis(
        (norm_train + norm_step).astype(jnp.bfloat16), SHARD_COLS, (3, 0, 1, 2), 0
    )
    return (serve_gate, serve_up, serve_norm)


def solution(mesh):
    finer = Mesh(
        mesh.devices.reshape(mesh.shape["trial"], 4, 4, 2, mesh.shape["cols"]),
        ("trial", "shard_0", "shard_1", "shard_2", "cols"),
    )
    in_specs = (
        P(TRIAL_SHARD, "cols"),
        P(TRIAL_SHARD, None),
        P("trial", "cols"),
        P(TRIAL_SHARD, "cols"),
        P(TRIAL_SHARD, None),
        P("trial", "cols"),
        P(TRIAL_SHARD_COLS),
        P(TRIAL_SHARD_COLS),
    )
    out_specs = (P(("trial", "cols"), None), P(("trial", "cols"), None), P("trial"))
    return jax.shard_map(local, mesh=finer, in_specs=in_specs, out_specs=out_specs, check_vma=False)
```

profile of v0, /device:TPU:1, one launch (start us, length us, event | category | flops | bytes accessed | tf_op | source)
XLA Modules:
  0.0 136.6 jit_solution(6419742506803516360)
XLA Ops:
  7.2 0.0 copy-start
  7.2 0.0 all-gather.7.cloned.1.call-start
  7.2 0.8 copy-done
  8.0 1.2 fusion.2
  9.2 1.2 fusion.3
  10.5 0.8 pad_maximum_fusion
  11.3 0.0 all-gather.7.cloned.1.call-update
  11.3 1.3 dynamic-slice
  13.3 0.7 add_convert_fusion
  13.9 0.2 dynamic-update-slice
  14.1 11.8 %all-reduce = bf16[64]{0:T(256)(128)(2,1)S(1)} all-reduce(bf16[64]{0:T(256)(128)(2,1)S(1)} %dynamic-update-slice), channel_id=2, replica_groups=mesh['trial'=2,'shard_0'=4,'shard_1'=4,'shard_2'=2,'cols'=4] {'cols'}, use_global_device_ids=true, to_apply=%add | all-reduce | flops 64 | bytes 256
  25.9 0.1 reshape.13
  26.0 8.5 %all-gather.4 = bf16[4,4,16]{2,1,0:T(4,128)(2,1)S(1)} all-gather(bf16[1,4,16]{2,1,0:T(4,128)(2,1)S(1)} %reshape.13), channel_id=3, replica_groups=mesh['trial'=2,'shard_0'=4,'shard_1'=4,'shard_2'=2,'cols'=4] {'shard_0'}, dimensions={0}, use_global_device_ids=true | all-gather | bytes 640 | tf_op jit(solution)/shard_map/all_gather | solution.py:34
  34.5 10.5 %all-gather.2 = bf16[16,4,16]{2,1,0:T(4,128)(2,1)S(1)} all-gather(bf16[4,4,16]{2,1,0:T(4,128)(2,1)S(1)} %all-gather.4), channel_id=4, replica_groups=mesh['trial'=2,'shard_0'=4,'shard_1'=4,'shard_2'=2,'cols'=4] {'shard_1'}, dimensions={0}, use_global_device_ids=true | all-gather | bytes 2560 | tf_op jit(solution)/shard_map/all_gather | solution.py:34
  45.0 7.5 %all-gather.3 = bf16[8,4,4,16]{3,2,1,0:T(4,128)(2,1)S(1)} all-gather(bf16[4,4,4,16]{3,2,1,0:T(4,128)(2,1)S(1)} %bitcast.14), channel_id=5, replica_groups=mesh['trial'=2,'shard_0'=4,'shard_1'=4,'shard_2'=2,'cols'=4] {'shard_2'}, dimensions={0}, use_global_device_ids=true | all-gather | bytes 6144 | tf_op jit(solution)/shard_map/all_gather | solution.py:34
  52.5 0.7 reshape_reshape.3
  53.2 40.1 %all-gather.7.cloned.1.call-done = bf16[2048,4096]{1,0:T(8,128)(2,1)} async-done(((bf16[64,4096]{1,0:T(8,128)(2,1)}), bf16[2048,4096]{1,0:T(8,128)(2,1)}) %all-gather.7.cloned.1.call-update) | async-done | bytes 16777232 | tf_op jit(solution)/shard_map/all_gather | solution.py:18
  93.3 11.9 %slice_bitcast_fusion = (bf16[2048,2048]{0,1:T(8,128)(2,1)}, bf16[2048,2048]{0,1:T(8,128)(2,1)}) fusion(bf16[2048,4096]{1,0:T(8,128)(2,1)} %all-gather.7.cloned.1.call-done), kind=kLoop, calls=%fused_computation | loop fusion | bytes 33554432 | tf_op jit(solution)/shard_map/transpose | solution.py:54
  105.3 12.2 %copy.21 = bf16[2048,2048]{1,0:T(8,128)(2,1)} copy(bf16[2048,2048]{0,1:T(8,128)(2,1)} %get-tuple-element.16) | data formatting | bytes 16777216
  117.5 12.2 %copy.22 = bf16[2048,2048]{1,0:T(8,128)(2,1)} copy(bf16[2048,2048]{0,1:T(8,128)(2,1)} %get-tuple-element.15) | data formatting | bytes 16777216
  (3 shorter events, 0.0 us)
Async XLA Ops:
  7.2 0.8 copy-start
  7.2 86.1 %all-gather.7.cloned.1.call-start = ((), (), s32[]{:S(2)}) async-start(), calls=%async_computation | async-start | bytes 17301504 | tf_op jit(solution)/shard_map/all_gather | solution.py:18
Sparse Core Ops, SparseCore 0:
  11.5 81.8 all-gather.6
where the time goes:
time: 137 us
  waiting for transfers between devices  40.1 us (29%)
  local copies, waits for them, and re-layouts  39.5 us (29%)
  blocking collectives  38.3 us (28%)
  between operations  14.7 us (11%)
  matrix products  2.46 us (2%)
  other arithmetic  1.51 us (1%)
    all_gather x1, waiting for transfers between devices, side_by_side(): lax.all_gather(both, axis, axis=dim, tiled=True)  40.1 us
    unnamed x8, local copies, waits for them, and re-layouts  26.8 us
    all_gather x3, blocking collectives, all_blocks(): tiles = lax.all_gather(tiles, axes[k])  26.5 us
    transpose x1, local copies, waits for them, and re-layouts, local(): serve_gate, serve_up = (serve_gate.T, serve_up.T)  11.9 us
    unnamed x1, blocking collectives  11.8 us
  transfers between devices with their start and end apart: 1, of which 1 were waited for; matrix products, arithmetic and copies ran while one was open for 2% of the time, Pallas kernels for 0%

commit v1 on v0

v1 whole, which is shorter than its diff:
```python
import functools

import jax
import jax.numpy as jnp
from jax import lax
from jax.experimental import pallas as pl
from jax.experimental.pallas import tpu as pltpu
from jax.sharding import Mesh
from jax.sharding import PartitionSpec as P

TRIAL_SHARD = ("trial", "y", "x", "core")
TRIAL_SHARD_COLS = ("trial", "y", "x", "core", "cols")
MESH_ID = pl.DeviceIdType.MESH
MIX_RATE = 2.0
SIDE = 4
CHIPS = SIDE * SIDE
LANES = 128


def fresh(train, low, high):
    return train[...].astype(jnp.float32) + MIX_RATE * jnp.dot(
        low[...], high[...], preferred_element_type=jnp.float32
    )


def gather_kernel(
    train_gate, low_gate, high_gate, train_up, low_up, high_up, norm_train, norm_step,
    gate, up, norm,
    gate_sent, gate_came, gate_gave, gate_got, up_sent, up_came, up_gave, up_got, norm_sent, norm_came,
):
    y, x, core, col = (lax.axis_index(a) for a in ("y", "x", "core", "cols"))
    sibling = 1 - core

    def wrap(i):
        return lax.rem(i + SIDE, SIDE)

    neighbours = [{"x": wrap(x + 1)}, {"x": wrap(x - 1)}, {"y": wrap(y + 1)}, {"y": wrap(y - 1)}]
    partners = [{"core": sibling}] + [{"cols": wrap(col + k)} for k in (1, 2, 3)]

    barrier = pltpu.get_barrier_semaphore()
    for device in neighbours + partners:
        pl.semaphore_signal(barrier, inc=1, device_id=device, device_id_type=MESH_ID)

    mine = y * SIDE + x
    gate[core, mine] = fresh(train_gate, low_gate, high_gate).astype(jnp.bfloat16)
    up[core, mine] = fresh(train_up, low_up, high_up).astype(jnp.bfloat16)
    lane = lax.broadcasted_iota(jnp.int32, (1, LANES), 1)
    row = jnp.zeros((1, LANES), jnp.float32)
    first = core * 64 + col * 16
    for i in range(16):
        row = jnp.where(lane == first + i, norm_train[i] + norm_step[i], row)
    norm[core, y, x, col] = row

    pl.semaphore_wait(barrier, len(neighbours + partners))

    def send(src, dst, sent, came, device):
        pltpu.make_async_remote_copy(
            src_ref=src, dst_ref=dst, send_sem=sent, recv_sem=came, device_id=device, device_id_type=MESH_ID
        ).start()

    def arrive(ref, sem):
        pltpu.make_async_copy(ref, ref, sem).wait()

    class Stream:
        def __init__(self, fast_is_x, ref, sent, came, gave, got):
            self.fast_is_x, self.ref = fast_is_x, ref
            self.sent, self.came, self.gave, self.took = sent, came, gave, got

        def chip(self, f, s):
            f, s = (wrap(f + x), wrap(s + y)) if self.fast_is_x else (wrap(f + y), wrap(s + x))
            return s * SIDE + f if self.fast_is_x else f * SIDE + s

        def device(self, along_fast, step):
            axis, at = ("x", x) if along_fast == self.fast_is_x else ("y", y)
            return {axis: wrap(at + step)}

        def block(self, f, s, half=None):
            rows = slice(None) if half is None else pl.ds(half * 32, 32)
            return self.ref.at[core, self.chip(f, s), rows]

        def push(self, along_fast, step, f, s, half, slot):
            piece = self.block(f, s, half)
            send(piece, piece, self.sent, self.came.at[slot], self.device(along_fast, step))

        def share(self, piece):
            send(piece, piece, self.gave, self.took, {"core": sibling})

        def got(self, f, s, half, slot):
            piece = self.block(f, s, half)
            arrive(piece, self.came.at[slot])
            self.share(piece)

    a = Stream(True, gate, gate_sent, gate_came, gate_gave, gate_got)
    b = Stream(False, up, up_sent, up_came, up_gave, up_got)
    both = (a, b)

    def fast_own(st):
        st.push(True, 1, 0, 0, None, 0)
        st.push(True, -1, 0, 0, None, 1)

    def fast_near(st):
        st.got(-1, 0, None, 0)
        st.push(True, 1, -1, 0, 0, 2)
        st.got(1, 0, None, 1)
        st.push(True, -1, 1, 0, 1, 3)

    def fast_far(st):
        st.got(2, 0, 0, 2)
        st.got(2, 0, 1, 3)

    def slow_own(st, f):
        k = 4 + 4 * (f % 4)
        st.push(False, 1, f, 0, None, k)
        st.push(False, -1, f, 0, None, k + 1)

    def slow_near(st, f):
        k = 4 + 4 * (f % 4)
        st.got(f, -1, None, k)
        st.push(False, 1, f, -1, 0, k + 2)
        st.got(f, 1, None, k + 1)
        st.push(False, -1, f, 1, 1, k + 3)

    def slow_far(st, f):
        k = 4 + 4 * (f % 4)
        st.got(f, 2, 0, k + 2)
        st.got(f, 2, 1, k + 3)

    own_norm = norm.at[core, y, x, col]
    for k in (1, 2, 3):
        send(own_norm, own_norm, norm_sent.at[k - 1], norm_came.at[k - 1], {"cols": wrap(col + k)})
    for st in both:
        fast_own(st)
    for st in both:
        slow_own(st, 0)
    for st in both:
        st.share(st.block(0, 0))

    for k in (1, 2, 3):
        arrive(norm.at[core, y, x, wrap(col - k)], norm_came.at[k - 1])
    own_norm = norm.at[core, y, x]
    send(own_norm, own_norm, norm_sent.at[3], norm_came.at[3], {"x": wrap(x + 1)})
    send(own_norm, own_norm, norm_sent.at[4], norm_came.at[4], {"x": wrap(x - 1)})

    for st in both:
        fast_near(st)
    arrive(norm.at[core, y, wrap(x - 1)], norm_came.at[3])
    arrive(norm.at[core, y, wrap(x + 1)], norm_came.at[4])
    far_norm = norm.at[core, y, wrap(x - 1)]
    send(far_norm, far_norm, norm_sent.at[5], norm_came.at[5], {"x": wrap(x + 1)})
    for f in (-1, 1):
        for st in both:
            slow_own(st, f)
    for st in both:
        slow_near(st, 0)
    arrive(norm.at[core, y, wrap(x + 2)], norm_came.at[5])
    norm_rows = norm.at[core, y]
    send(norm_rows, norm_rows, norm_sent.at[6], norm_came.at[6], {"y": wrap(y + 1)})
    send(norm_rows, norm_rows, norm_sent.at[7], norm_came.at[7], {"y": wrap(y - 1)})
    for st in both:
        fast_far(st)
    for st in both:
        slow_own(st, 2)
    for f in (-1, 1):
        for st in both:
            slow_near(st, f)
    arrive(norm.at[core, wrap(y - 1)], norm_came.at[6])
    arrive(norm.at[core, wrap(y + 1)], norm_came.at[7])
    far_rows = norm.at[core, wrap(y - 1)]
    send(far_rows, far_rows, norm_sent.at[8], norm_came.at[8], {"y": wrap(y + 1)})
    for st in both:
        slow_far(st, 0)
    for f in (-1, 1):
        for st in both:
            slow_far(st, f)
    arrive(norm.at[core, wrap(y + 2)], norm_came.at[8])
    send(norm.at[core], norm.at[core], norm_sent.at[9], norm_came.at[9], {"core": sibling})
    for st in both:
        slow_near(st, 2)
    for st in both:
        slow_far(st, 2)

    for st in both:
        arrive(st.ref.at[core, pl.ds(0, 15)], st.sent)
        arrive(st.ref.at[core], st.gave)
        arrive(st.ref.at[sibling], st.took)
    for k in range(3):
        arrive(norm.at[core, y, x, col], norm_sent.at[k])
    for k in range(3, 6):
        arrive(norm.at[core, y, x], norm_sent.at[k])
    for k in range(6, 9):
        arrive(norm.at[core, y], norm_sent.at[k])
    arrive(norm.at[core], norm_sent.at[9])
    arrive(norm.at[sibling], norm_came.at[9])


def gather(train_gate, low_gate, high_gate, train_up, low_up, high_up, norm_train, norm_step):
    rows, width = train_gate.shape
    vmem = pl.BlockSpec(memory_space=pltpu.VMEM)
    smem = pl.BlockSpec(memory_space=pltpu.SMEM)
    dma = pltpu.SemaphoreType.DMA
    return pl.pallas_call(
        gather_kernel,
        name="gather",
        out_shape=(
            pltpu.VMEM((2, CHIPS, rows, width), jnp.bfloat16),
            pltpu.VMEM((2, CHIPS, rows, width), jnp.bfloat16),
            pltpu.VMEM((2, SIDE, SIDE, SIDE, 1, LANES), jnp.float32),
        ),
        in_specs=[vmem] * 6 + [smem] * 2,
        out_specs=(vmem, vmem, vmem),
        scratch_shapes=[dma, dma((20,)), dma, dma] * 2 + [dma((10,)), dma((10,))],
        compiler_params=pltpu.CompilerParams(
            collective_id=0, has_side_effects=True, vmem_limit_bytes=24 * 2**20
        ),
    )(train_gate, low_gate, high_gate, train_up, low_up, high_up, norm_train, norm_step)


STEP = 256
SLOTS = 4


def finish_kernel(gate, up, norm, serve_gate, serve_up, serve_norm, rows, sems):
    serve_norm[...] = jnp.sum(norm[...], axis=(0, 3)).reshape(CHIPS, LANES).astype(jnp.bfloat16)
    steps = gate.shape[-1] // STEP

    def flush(out, i, slot):
        return pltpu.make_async_copy(rows.at[slot], out.at[pl.ds(i * STEP, STEP)], sems.at[slot])

    jobs = [(src, out, i) for src, out in ((gate, serve_gate), (up, serve_up)) for i in range(steps)]
    for n, (src, out, i) in enumerate(jobs):
        slot = n % SLOTS
        if n >= SLOTS:
            flush(*jobs[n - SLOTS][1:], slot).wait()
        for k in range(CHIPS):
            tile = jnp.concatenate(
                [src[0, k, :, pl.ds(i * STEP, STEP)], src[1, k, :, pl.ds(i * STEP, STEP)]], axis=0
            )
            rows[slot, :, pl.ds(k * LANES, LANES)] = tile.T
        flush(out, i, slot).start()
    for n in range(len(jobs) - SLOTS, len(jobs)):
        flush(*jobs[n][1:], n % SLOTS).wait()


def finish(gate, up, norm):
    rows, width = gate.shape[-2:]
    vmem = pl.BlockSpec(memory_space=pltpu.VMEM)
    hbm = pl.BlockSpec(memory_space=pl.ANY)
    wide = 2 * CHIPS * rows
    return pl.pallas_call(
        finish_kernel,
        name="finish",
        out_shape=(
            jax.ShapeDtypeStruct((width, wide), jnp.bfloat16),
            jax.ShapeDtypeStruct((width, wide), jnp.bfloat16),
            jax.ShapeDtypeStruct((CHIPS, LANES), jnp.bfloat16),
        ),
        in_specs=[vmem] * 3,
        out_specs=(hbm, hbm, vmem),
        scratch_shapes=[pltpu.VMEM((SLOTS, STEP, wide), jnp.bfloat16), pltpu.SemaphoreType.DMA((SLOTS,))],
        compiler_params=pltpu.CompilerParams(vmem_limit_bytes=24 * 2**20),
    )(gate, up, norm)


def local(*args):
    serve_gate, serve_up, serve_norm = finish(*gather(*args))
    return serve_gate, serve_up, serve_norm.reshape(-1)


def solution(mesh):
    finer = Mesh(
        mesh.devices.reshape(mesh.shape["trial"], SIDE, SIDE, 2, mesh.shape["cols"]),
        ("trial", "y", "x", "core", "cols"),
    )
    in_specs = (
        P(TRIAL_SHARD, "cols"),
        P(TRIAL_SHARD, None),
        P("trial", "cols"),
        P(TRIAL_SHARD, "cols"),
        P(TRIAL_SHARD, None),
        P("trial", "cols"),
        P(TRIAL_SHARD_COLS),
        P(TRIAL_SHARD_COLS),
    )
    out_specs = (P(("trial", "cols"), None), P(("trial", "cols"), None), P("trial"))
    return jax.shard_map(local, mesh=finer, in_specs=in_specs, out_specs=out_specs, check_vma=False)
```

time: 137 us -> 72.1 us (0.53)
  Pallas kernels: 0 us -> 64.6 us
  waiting for transfers between devices: 40.1 us -> 0 us
  blocking collectives: 38.3 us -> 0 us
  local copies, waits for them, and re-layouts: 39.5 us -> 6.45 us
  between operations: 14.7 us -> 0.65 us
  matrix products: 2.46 us -> 0 us
  other arithmetic: 1.51 us -> 0 us
    pallas_call x0 -> x2, Pallas kernels: none -> 64.6 us  [the longest x1 57.3 us: gather(): pl.pallas_call(gather_kernel, name='gather', out_shape=(pltpu.VMEM((2, CH...]
    all_gather x1 -> x0, waiting for transfers between devices: 40.1 us -> none  [side_by_side(): lax.all_gather(both, axis, axis=dim, tiled=True)]
    all_gather x3 -> x0, blocking collectives: 26.5 us -> none  [all_blocks(): tiles = lax.all_gather(tiles, axes[k])]
    unnamed x8 -> x14, local copies, waits for them, and re-layouts: 26.8 us -> 6.45 us
    transpose x2 -> x0, local copies, waits for them, and re-layouts: 12 us -> none  [the longest x1 11.9 us: local(): serve_gate, serve_up = (serve_gate.T, serve_up.T)]
    unnamed x1 -> x0, blocking collectives: 11.8 us -> none
    dot_general x2 -> x0, matrix products: 2.46 us -> none  [the longest x1 1.25 us: local(): jnp.dot(low_up, high_up, preferred_element_type=jnp.float32)]
  transfers between devices with their start and end apart: 1 -> 0, of which waited for: 1 -> 0; matrix products, arithmetic and copies ran while one was open for 2% -> 0% of each run, Pallas kernels for 0% -> 0%
where the time goes in v1:
time: 72.1 us; the launch traced here: 71.7 us
  Pallas kernels  64.6 us (90%)
  local copies, waits for them, and re-layouts  6.45 us (9%)
    pallas_call x1, Pallas kernels, gather(): pl.pallas_call(gather_kernel, name='gather', out_shape=(pltpu.VMEM((2, CH...  57.3 us
    pallas_call x1, Pallas kernels, finish(): pl.pallas_call(finish_kernel, name='finish', out_shape=(jax.ShapeDtypeStr...  7.36 us
    unnamed x14, local copies, waits for them, and re-layouts  6.45 us

profile of v1, /device:TPU:1, one launch (start us, length us, event | category | flops | bytes accessed | tf_op | source)
XLA Modules:
  0.0 71.7 jit_solution(17202184392344144721)
XLA Ops:
  0.6 0.8 %copy.11.low_gate = bf16[64,16]{1,0:T(8,128)(2,1)S(1)} copy(bf16[64,16]{0,1:T(8,128)(2,1)} %param.9) | data formatting | bytes 4096 | tf_op args[1]
  1.4 0.8 %copy.12.low_up = bf16[64,16]{1,0:T(8,128)(2,1)S(1)} copy(bf16[64,16]{0,1:T(8,128)(2,1)} %param.12) | data formatting | bytes 4096 | tf_op args[4]
  2.2 0.0 copy-start
  2.2 0.9 %copy-done = bf16[64,2048]{1,0:T(8,128)(2,1)S(1)} copy-done((bf16[64,2048]{1,0:T(8,128)(2,1)S(1)}, bf16[64,2048]{1,0:T(8,128)(2,1)}, u32[]{:S(2)}) %copy-start) | copy-done | bytes 262168
  3.1 0.0 copy-start.1
  3.1 0.9 %copy-done.1 = bf16[64,2048]{1,0:T(8,128)(2,1)S(1)} copy-done((bf16[64,2048]{1,0:T(8,128)(2,1)S(1)}, bf16[64,2048]{1,0:T(8,128)(2,1)}, u32[]{:S(2)}) %copy-start.1) | copy-done | bytes 262168
  4.1 0.0 copy-start.2
  4.1 0.8 %copy-done.2 = bf16[16,2048]{1,0:T(8,128)(2,1)S(1)} copy-done((bf16[16,2048]{1,0:T(8,128)(2,1)S(1)}, bf16[16,2048]{1,0:T(8,128)(2,1)}, u32[]{:S(2)}) %copy-start.2) | copy-done | bytes 65560
  4.9 0.0 copy-start.3
  4.9 0.8 %copy-done.3 = bf16[16,2048]{1,0:T(8,128)(2,1)S(1)} copy-done((bf16[16,2048]{1,0:T(8,128)(2,1)S(1)}, bf16[16,2048]{1,0:T(8,128)(2,1)}, u32[]{:S(2)}) %copy-start.3) | copy-done | bytes 65560
  5.8 0.0 copy-start.4
  5.8 0.7 copy-done.4
  6.4 0.0 copy-start.5
  6.4 0.7 copy-done.5
  7.1 57.3 %gather.1 = (bf16[2,16,64,2048]{3,2,1,0:T(8,128)(2,1)S(1)}, bf16[2,16,64,2048]{3,2,1,0:T(8,128)(2,1)S(1)}, f32[2,4,4,4,1,128]{5,4,3,2,1,0:T(1,128)S(1)}) custom-call(bf16[64,2048]{1,0:T(8,128)(2,1)S(1)} %copy-done, bf16[64,16]{1,0:T(8,128)(2,1)S(1)} %copy.11.low_gate, bf16[16,2048]{1,0:T(8,128)(2,1)S(1)} %copy-done.2, bf16[64,2048]{1,0:T(8,128)(2,1)S(1)} %copy-done.1, ...), custom_call_target="tpu_custom_call" | custom-call | tf_op jit(solution)/shard_map/gather/pallas_call | solution.py:201
  64.4 7.4 %finish.1 = (bf16[2048,2048]{1,0:T(8,128)(2,1)}, bf16[2048,2048]{1,0:T(8,128)(2,1)}, bf16[16,128]{1,0:T(8,128)(2,1)}) custom-call(bf16[2,16,64,2048]{3,2,1,0:T(8,128)(2,1)S(1)} %get-tuple-element.9.gate, bf16[2,16,64,2048]{3,2,1,0:T(8,128)(2,1)S(1)} %get-tuple-element.10.up, f32[2,4,4,4,1,128]{5,4,3,2,1,0:T(1,128)S(1)} %get-tuple-element.11.norm), custom_call_target="tpu_custom_call" | custom-call | tf_op jit(solution)/shard_map/finish/pallas_call | solution.py:249
Async XLA Ops:
  2.2 1.0 %copy-start = (bf16[64,2048]{1,0:T(8,128)(2,1)S(1)}, bf16[64,2048]{1,0:T(8,128)(2,1)}, u32[]{:S(2)}) copy-start(bf16[64,2048]{1,0:T(8,128)(2,1)} %train_gate.1) | copy-start | bytes 786436
  3.1 0.9 %copy-start.1 = (bf16[64,2048]{1,0:T(8,128)(2,1)S(1)}, bf16[64,2048]{1,0:T(8,128)(2,1)}, u32[]{:S(2)}) copy-start(bf16[64,2048]{1,0:T(8,128)(2,1)} %train_up.1) | copy-start | bytes 786436
  4.1 0.8 %copy-start.2 = (bf16[16,2048]{1,0:T(8,128)(2,1)S(1)}, bf16[16,2048]{1,0:T(8,128)(2,1)}, u32[]{:S(2)}) copy-start(bf16[16,2048]{1,0:T(8,128)(2,1)} %high_gate.1) | copy-start | bytes 196612
  4.9 0.8 %copy-start.3 = (bf16[16,2048]{1,0:T(8,128)(2,1)S(1)}, bf16[16,2048]{1,0:T(8,128)(2,1)}, u32[]{:S(2)}) copy-start(bf16[16,2048]{1,0:T(8,128)(2,1)} %high_up.1) | copy-start | bytes 196612
  5.8 0.7 copy-start.4
  6.4 0.7 copy-start.5

commit v2 on v1

v2 whole, which is shorter than its diff:
```python
import functools

import jax
import jax.numpy as jnp
from jax import lax
from jax.experimental import pallas as pl
from jax.experimental.pallas import tpu as pltpu
from jax.sharding import Mesh
from jax.sharding import PartitionSpec as P

TRIAL_SHARD = ("trial", "y", "x", "core")
TRIAL_SHARD_COLS = ("trial", "y", "x", "core", "cols")
MESH_ID = pl.DeviceIdType.MESH
MIX_RATE = 2.0
SIDE = 4
CHIPS = SIDE * SIDE
LANES = 128


def gather_kernel(
    train_gate, low_gate, high_gate, train_up, low_up, high_up, norm_train, norm_step,
    gate, up, norm,
    train, low, high, gain, loaded,
    gate_sent, gate_came, gate_gave, gate_took, up_sent, up_came, up_gave, up_took, norm_sent, norm_came,
):
    y, x, core, col = (lax.axis_index(a) for a in ("y", "x", "core", "cols"))
    sibling = 1 - core

    def wrap(i):
        return lax.rem(i + SIDE, SIDE)

    barrier = pltpu.get_barrier_semaphore()
    partners = [{"cols": wrap(col + k)} for k in (2, 1, 3)]
    partners += [{"x": wrap(x + 1)}, {"x": wrap(x - 1)}, {"y": wrap(y + 1)}, {"y": wrap(y - 1)}, {"core": sibling}]
    for device in partners:
        pl.semaphore_signal(barrier, inc=1, device_id=device, device_id_type=MESH_ID)

    pairs = [
        (train_gate, train.at[0]), (low_gate, low.at[0]), (high_gate, high.at[0]),
        (train_up, train.at[1]), (low_up, low.at[1]), (high_up, high.at[1]),
        (norm_train, gain.at[0]), (norm_step, gain.at[1]),
    ]
    loads = [pltpu.make_async_copy(src, dst, loaded.at[k]) for k, (src, dst) in enumerate(pairs)]
    for load in loads:
        load.start()

    mine = y * SIDE + x
    for k, ref in enumerate((gate, up)):
        for load in loads[3 * k : 3 * k + 3]:
            load.wait()
        product = lax.dot_general(
            low[k], high[k], (((0,), (0,)), ((), ())), preferred_element_type=jnp.float32
        )
        ref[core, mine] = (train[k].astype(jnp.float32) + MIX_RATE * product).astype(jnp.bfloat16)
    for load in loads[6:]:
        load.wait()
    lane = lax.broadcasted_iota(jnp.int32, (1, LANES), 1)
    row = jnp.zeros((1, LANES), jnp.float32)
    first = core * 64 + col * 16
    for i in range(16):
        row = jnp.where(lane == first + i, gain[0, i] + gain[1, i], row)
    norm[core, y, x, col] = row

    pl.semaphore_wait(barrier, len(partners))

    def send(piece, sent, came, device):
        pltpu.make_async_remote_copy(
            src_ref=piece, dst_ref=piece, send_sem=sent, recv_sem=came, device_id=device, device_id_type=MESH_ID
        ).start()

    def arrive(piece, sem):
        pltpu.make_async_copy(piece, piece, sem).wait()

    class Stream:
        def __init__(self, fast_is_x, ref, sent, came, gave, took):
            self.fast_is_x, self.ref = fast_is_x, ref
            self.sent, self.came, self.gave, self.took = sent, came, gave, took

        def block(self, f, s, half=None):
            at_x, at_y = (x + f, y + s) if self.fast_is_x else (x + s, y + f)
            rows = slice(None) if half is None else pl.ds(half * 32, 32)
            return self.ref.at[core, wrap(at_y) * SIDE + wrap(at_x), rows]

        def push(self, along_fast, step, piece, slot):
            axis, at = ("x", x) if along_fast == self.fast_is_x else ("y", y)
            send(piece, self.sent, self.came.at[slot], {axis: wrap(at + step)})

        def share(self, piece):
            send(piece, self.gave, self.took, {"core": sibling})

        def got(self, piece, slot):
            arrive(piece, self.came.at[slot])
            self.share(piece)

        def fast_own(self):
            self.push(True, 1, self.block(0, 0), 0)
            self.push(True, -1, self.block(0, 0), 1)

        def fast_near(self):
            self.got(self.block(-1, 0), 0)
            self.push(True, 1, self.block(-1, 0, 0), 2)
            self.got(self.block(1, 0), 1)
            self.push(True, -1, self.block(1, 0, 1), 3)

        def fast_far(self):
            self.got(self.block(2, 0, 0), 2)
            self.got(self.block(2, 0, 1), 3)

        def slow_own(self, f):
            k = 4 + 4 * (f % SIDE)
            self.push(False, 1, self.block(f, 0), k)
            self.push(False, -1, self.block(f, 0), k + 1)

        def slow_near(self, f):
            k = 4 + 4 * (f % SIDE)
            self.got(self.block(f, -1), k)
            self.got(self.block(f, 1), k + 1)

        def slow_pass(self, f):
            k = 4 + 4 * (f % SIDE)
            self.push(False, 1, self.block(f, -1, 0), k + 2)
            self.push(False, -1, self.block(f, 1, 1), k + 3)

        def slow_far(self, f):
            k = 4 + 4 * (f % SIDE)
            self.got(self.block(f, 2, 0), k + 2)
            self.got(self.block(f, 2, 1), k + 3)

    streams = (
        Stream(True, gate, gate_sent, gate_came, gate_gave, gate_took),
        Stream(False, up, up_sent, up_came, up_gave, up_took),
    )

    def each(method, *args):
        for st in streams:
            getattr(st, method)(*args)

    def norm_send(piece, axis, at, slot):
        for k in (1, 2, 3):
            send(piece, norm_sent.at[slot + k - 1], norm_came.at[slot + k - 1], {axis: wrap(at + k)})

    def norm_arrive(at, piece_at, slot):
        for k in (1, 2, 3):
            arrive(piece_at(wrap(at - k)), norm_came.at[slot + k - 1])

    each("fast_own")
    each("slow_own", 0)
    norm_send(norm.at[core, y, x, col], "cols", col, 0)
    for st in streams:
        st.share(st.block(0, 0))
    each("fast_near")
    norm_arrive(col, lambda i: norm.at[core, y, x, i], 0)
    norm_send(norm.at[core, y, x], "x", x, 3)
    each("slow_own", -1)
    each("slow_own", 1)
    each("slow_near", 0)
    each("fast_far")
    each("slow_own", 2)
    each("slow_pass", 0)
    each("slow_near", -1)
    norm_arrive(x, lambda i: norm.at[core, y, i], 3)
    norm_send(norm.at[core, y], "y", y, 6)
    each("slow_pass", -1)
    each("slow_near", 1)
    each("slow_pass", 1)
    each("slow_near", 2)
    each("slow_pass", 2)
    each("slow_far", 0)
    each("slow_far", -1)
    norm_arrive(y, lambda i: norm.at[core, i], 6)
    send(norm.at[core], norm_sent.at[9], norm_came.at[9], {"core": sibling})
    each("slow_far", 1)
    each("slow_far", 2)

    for st in streams:
        arrive(st.ref.at[core, pl.ds(0, 15)], st.sent)
        arrive(st.ref.at[core], st.gave)
    for piece, slot in ((norm.at[core, y, x, col], 0), (norm.at[core, y, x], 3), (norm.at[core, y], 6)):
        for k in range(3):
            arrive(piece, norm_sent.at[slot + k])
    arrive(norm.at[core], norm_sent.at[9])
    arrive(norm.at[sibling], norm_came.at[9])
    for st in streams:
        arrive(st.ref.at[sibling], st.took)


def gather(train_gate, low_gate, high_gate, train_up, low_up, high_up, norm_train, norm_step):
    rows, width = train_gate.shape
    rank = low_gate.shape[1]
    vmem = pl.BlockSpec(memory_space=pltpu.VMEM)
    hbm = pl.BlockSpec(memory_space=pltpu.HBM)
    dma = pltpu.SemaphoreType.DMA
    return pl.pallas_call(
        gather_kernel,
        name="gather",
        out_shape=(
            pltpu.VMEM((2, CHIPS, rows, width), jnp.bfloat16),
            pltpu.VMEM((2, CHIPS, rows, width), jnp.bfloat16),
            pltpu.VMEM((2, SIDE, SIDE, SIDE, 1, LANES), jnp.float32),
        ),
        in_specs=[hbm] * 8,
        out_specs=(vmem, vmem, vmem),
        scratch_shapes=[
            pltpu.VMEM((2, rows, width), jnp.bfloat16),
            pltpu.VMEM((2, rank, rows), jnp.bfloat16),
            pltpu.VMEM((2, rank, width), jnp.bfloat16),
            pltpu.SMEM((2, 16), jnp.float32),
            dma((8,)),
        ]
        + [dma, dma((20,)), dma, dma] * 2
        + [dma((10,)), dma((10,))],
        compiler_params=pltpu.CompilerParams(
            collective_id=0, has_side_effects=True, vmem_limit_bytes=24 * 2**20
        ),
    )(*(
        pltpu.with_memory_space_constraint(a, pltpu.HBM)
        for a in (train_gate, low_gate.T, high_gate, train_up, low_up.T, high_up, norm_train, norm_step)
    ))


STEP = 256
SLOTS = 4


def finish_kernel(gate, up, norm, serve_gate, serve_up, serve_norm, rows, sems):
    steps = gate.shape[-1] // STEP

    def flush(out, i, slot):
        return pltpu.make_async_copy(rows.at[slot], out.at[pl.ds(i * STEP, STEP)], sems.at[slot])

    jobs = [(src, out, i) for src, out in ((gate, serve_gate), (up, serve_up)) for i in range(steps)]
    for n, (src, out, i) in enumerate(jobs):
        slot = n % SLOTS
        if n >= SLOTS:
            flush(*jobs[n - SLOTS][1:], slot).wait()
        for k in range(CHIPS):
            tile = jnp.concatenate(
                [src[0, k, :, pl.ds(i * STEP, STEP)], src[1, k, :, pl.ds(i * STEP, STEP)]], axis=0
            )
            rows[slot, :, pl.ds(k * LANES, LANES)] = tile.T
        flush(out, i, slot).start()
    serve_norm[...] = jnp.sum(norm[...], axis=(0, 3)).reshape(CHIPS, LANES).astype(jnp.bfloat16)
    for n in range(len(jobs) - SLOTS, len(jobs)):
        flush(*jobs[n][1:], n % SLOTS).wait()


def finish(gate, up, norm):
    rows, width = gate.shape[-2:]
    vmem = pl.BlockSpec(memory_space=pltpu.VMEM)
    hbm = pl.BlockSpec(memory_space=pl.ANY)
    wide = 2 * CHIPS * rows
    return pl.pallas_call(
        finish_kernel,
        name="finish",
        out_shape=(
            jax.ShapeDtypeStruct((width, wide), jnp.bfloat16),
            jax.ShapeDtypeStruct((width, wide), jnp.bfloat16),
            jax.ShapeDtypeStruct((CHIPS, LANES), jnp.bfloat16),
        ),
        in_specs=[vmem] * 3,
        out_specs=(hbm, hbm, vmem),
        scratch_shapes=[pltpu.VMEM((SLOTS, STEP, wide), jnp.bfloat16), pltpu.SemaphoreType.DMA((SLOTS,))],
        compiler_params=pltpu.CompilerParams(vmem_limit_bytes=24 * 2**20),
    )(gate, up, norm)


def local(*args):
    serve_gate, serve_up, serve_norm = finish(*gather(*args))
    return serve_gate, serve_up, serve_norm.reshape(-1)


def solution(mesh):
    finer = Mesh(
        mesh.devices.reshape(mesh.shape["trial"], SIDE, SIDE, 2, mesh.shape["cols"]),
        ("trial", "y", "x", "core", "cols"),
    )
    in_specs = (
        P(TRIAL_SHARD, "cols"),
        P(TRIAL_SHARD, None),
        P("trial", "cols"),
        P(TRIAL_SHARD, "cols"),
        P(TRIAL_SHARD, None),
        P("trial", "cols"),
        P(TRIAL_SHARD_COLS),
        P(TRIAL_SHARD_COLS),
    )
    out_specs = (P(("trial", "cols"), None), P(("trial", "cols"), None), P("trial"))
    return jax.shard_map(local, mesh=finer, in_specs=in_specs, out_specs=out_specs, check_vma=False)
```

time: 72.1 us -> 62.4 us (0.87)
  local copies, waits for them, and re-layouts: 6.45 us -> 0 us
  Pallas kernels: 64.6 us -> 61.7 us
    unnamed x14 -> x0, local copies, waits for them, and re-layouts: 6.45 us -> none
    pallas_call x1, Pallas kernels: 57.3 us -> 54.3 us  [gather(): pl.pallas_call(gather_kernel, name='gather', out_shape=(pltpu.VMEM((2, CH...]
where the time goes in v2:
time: 62.4 us; the launch traced here: 62.3 us
  Pallas kernels  61.7 us (99%)
  between operations  0.64 us (1%)
    pallas_call x1, Pallas kernels, gather(): pl.pallas_call(gather_kernel, name='gather', out_shape=(pltpu.VMEM((2, CH...  54.3 us
    pallas_call x1, Pallas kernels, finish(): pl.pallas_call(finish_kernel, name='finish', out_shape=(jax.ShapeDtypeStr...  7.4 us

profile of v2, /device:TPU:1, one launch (start us, length us, event | category | flops | bytes accessed | tf_op | source)
XLA Modules:
  0.0 62.3 jit_solution(7938659257256806096)
XLA Ops:
  0.6 54.3 %gather.1 = (bf16[2,16,64,2048]{3,2,1,0:T(8,128)(2,1)S(1)}, bf16[2,16,64,2048]{3,2,1,0:T(8,128)(2,1)S(1)}, f32[2,4,4,4,1,128]{5,4,3,2,1,0:T(1,128)S(1)}) custom-call(bf16[64,2048]{1,0:T(8,128)(2,1)} %train_gate.1, bf16[16,64]{1,0:T(8,128)(2,1)} %bitcast.3, bf16[16,2048]{1,0:T(8,128)(2,1)} %high_gate.1, bf16[64,2048]{1,0:T(8,128)(2,1)} %train_up.1, ...), custom_call_target="tpu_custom_call" | custom-call | tf_op jit(solution)/shard_map/gather/pallas_call | solution.py:193
  54.9 7.4 %finish.1 = (bf16[2048,2048]{1,0:T(8,128)(2,1)}, bf16[2048,2048]{1,0:T(8,128)(2,1)}, bf16[16,128]{1,0:T(8,128)(2,1)}) custom-call(bf16[2,16,64,2048]{3,2,1,0:T(8,128)(2,1)S(1)} %get-tuple-element.9.gate, bf16[2,16,64,2048]{3,2,1,0:T(8,128)(2,1)S(1)} %get-tuple-element.10.up, f32[2,4,4,4,1,128]{5,4,3,2,1,0:T(1,128)S(1)} %get-tuple-element.11.norm), custom_call_target="tpu_custom_call" | custom-call | tf_op jit(solution)/shard_map/finish/pallas_call | solution.py:252

commit v3 on v2

v3 whole, which is shorter than its diff:
```python
import functools

import jax
import jax.numpy as jnp
from jax import lax
from jax.experimental import pallas as pl
from jax.experimental.pallas import tpu as pltpu
from jax.sharding import Mesh
from jax.sharding import PartitionSpec as P

TRIAL_SHARD = ("trial", "y", "x", "core")
TRIAL_SHARD_COLS = ("trial", "y", "x", "core", "cols")
MESH_ID = pl.DeviceIdType.MESH
MIX_RATE = 2.0
SIDE = 4
CHIPS = SIDE * SIDE
LANES = 128


def gather_kernel(
    train_gate, low_gate, high_gate, train_up, low_up, high_up, norm_train, norm_step,
    turned, norm,
    train, low, high, gain, land, loaded, sent, came, gave, took, norm_sent, norm_came,
):
    y, x, core, col = (lax.axis_index(a) for a in ("y", "x", "core", "cols"))
    sibling = 1 - core

    def wrap(i):
        return lax.rem(i + SIDE, SIDE)

    beside, across = col + 1 - 2 * lax.rem(col, 2), wrap(col + 2)
    barrier = pltpu.get_barrier_semaphore()
    partners = [{"cols": across}, {"cols": beside}]
    partners += [{"x": wrap(x + 1)}, {"x": wrap(x - 1)}, {"y": wrap(y + 1)}, {"y": wrap(y - 1)}, {"core": sibling}]
    for device in partners:
        pl.semaphore_signal(barrier, inc=1, device_id=device, device_id_type=MESH_ID)

    pairs = [
        (train_gate, train.at[0]), (low_gate, low.at[0]), (high_gate, high.at[0]),
        (train_up, train.at[1]), (low_up, low.at[1]), (high_up, high.at[1]),
        (norm_train, gain.at[0]), (norm_step, gain.at[1]),
    ]
    loads = [pltpu.make_async_copy(src, dst, loaded.at[k]) for k, (src, dst) in enumerate(pairs)]
    for load in loads:
        load.start()

    mine = y * SIDE + x
    for k in range(2):
        for load in loads[3 * k : 3 * k + 3]:
            load.wait()
        product = lax.dot_general(
            low[k], high[k], (((0,), (0,)), ((), ())), preferred_element_type=jnp.float32
        )
        land[k, core, mine] = (train[k].astype(jnp.float32) + MIX_RATE * product).astype(jnp.bfloat16)
    for load in loads[6:]:
        load.wait()
    lane = lax.broadcasted_iota(jnp.int32, (1, LANES), 1)
    row = jnp.zeros((1, LANES), jnp.float32)
    first = core * 64 + col * 16
    for i in range(16):
        row = jnp.where(lane == first + i, gain[0, i] + gain[1, i], row)
    norm[core, y, x, col] = row

    pl.semaphore_wait(barrier, len(partners))

    def send(piece, sent_sem, came_sem, device):
        pltpu.make_async_remote_copy(
            src_ref=piece, dst_ref=piece, send_sem=sent_sem, recv_sem=came_sem, device_id=device, device_id_type=MESH_ID
        ).start()

    def arrive(piece, sem):
        pltpu.make_async_copy(piece, piece, sem).wait()

    def place(k, f, s):
        at_x, at_y = (x + f, y + s) if k == 0 else (x + s, y + f)
        return wrap(at_y) * SIDE + wrap(at_x)

    def block(k, f, s, at=0, rows=64):
        return land.at[k, core, place(k, f, s), pl.ds(at, rows)]

    def push(k, along_fast, step, piece, slot):
        axis, at = ("x", x) if along_fast == (k == 0) else ("y", y)
        send(piece, sent.at[k], came.at[k, slot], {axis: wrap(at + step)})

    def share(k, piece, group):
        send(piece, gave.at[k], took.at[k, group], {"core": sibling})

    def got(k, piece, slot, group):
        arrive(piece, came.at[k, slot])
        share(k, piece, group)

    def fast_own(k):
        push(k, True, 1, block(k, 0, 0), 0)
        push(k, True, -1, block(k, 0, 0), 1)

    def fast_near(k):
        got(k, block(k, -1, 0), 0, 0)
        push(k, True, 1, block(k, -1, 0, 0, 32), 2)
        got(k, block(k, 1, 0), 1, 0)
        push(k, True, -1, block(k, 1, 0, 32, 32), 3)

    def fast_far(k):
        got(k, block(k, 2, 0, 0, 32), 2, 0)
        got(k, block(k, 2, 0, 32, 32), 3, 0)

    def slow_own(k, f):
        slot = 4 + 4 * (f % SIDE)
        push(k, False, 1, block(k, f, 0), slot)
        push(k, False, -1, block(k, f, 0), slot + 1)

    def slow_near(k, f):
        slot = 4 + 4 * (f % SIDE)
        got(k, block(k, f, -1), slot, 1 + f % SIDE)
        got(k, block(k, f, 1), slot + 1, 1 + f % SIDE)

    def halves(f):
        slot = 4 + 4 * (f % SIDE)
        if f != 2:
            return [(0, 32, slot + 2, 1), (32, 32, slot + 3, -1)]
        return [(0, 16, slot + 2, 1), (32, 16, slot + 3, -1), (16, 16, 20, 1), (48, 16, 21, -1)]

    def slow_pass(k, f):
        for at, rows, slot, step in halves(f):
            push(k, False, step, block(k, f, -step, at, rows), slot)

    def slow_far(k, f):
        for at, rows, slot, _ in halves(f):
            got(k, block(k, f, 2, at, rows), slot, 5 + f % SIDE)

    def each(step, *args):
        for k in range(2):
            step(k, *args)

    def turn(group, chips):
        for k in range(2):
            arrive(land.at[k, sibling, pl.ds(0, len(chips))], took.at[k, group])
            for f, s in chips:
                chip = place(k, f, s)
                lanes = pl.ds(pl.multiple_of(chip * LANES, LANES), LANES)
                tile = jnp.concatenate([land[k, 0, chip], land[k, 1, chip]], axis=0)
                turned[k, :, lanes] = tile.T

    def norm_send(piece, axis, at, slot):
        for k in (1, 2, 3):
            send(piece, norm_sent.at[slot + k - 1], norm_came.at[slot + k - 1], {axis: wrap(at + k)})

    def norm_arrive(at, piece_at, slot):
        for k in (1, 2, 3):
            arrive(piece_at(wrap(at - k)), norm_came.at[slot + k - 1])

    one = norm.at[core, y, x, col]
    pair = norm.at[core, y, x, pl.ds(col - lax.rem(col, 2), 2)]
    other_pair = norm.at[core, y, x, pl.ds(across - lax.rem(across, 2), 2)]
    line, plane = norm.at[core, y, x], norm.at[core, y]

    each(fast_own)
    send(one, norm_sent.at[0], norm_came.at[0], {"cols": beside})
    each(slow_own, 0)
    each(lambda k: share(k, block(k, 0, 0), 0))
    arrive(norm.at[core, y, x, beside], norm_came.at[0])
    send(pair, norm_sent.at[1], norm_came.at[1], {"cols": across})
    each(fast_near)
    arrive(other_pair, norm_came.at[1])
    norm_send(line, "x", x, 2)
    each(slow_own, -1)
    each(slow_own, 1)
    each(slow_near, 0)
    each(fast_far)
    each(slow_own, 2)
    each(slow_pass, 0)
    each(slow_near, -1)
    norm_arrive(x, lambda i: norm.at[core, y, i], 2)
    norm_send(plane, "y", y, 5)
    each(slow_pass, -1)
    turn(0, [(0, 0), (-1, 0), (1, 0), (2, 0)])
    each(slow_near, 1)
    each(slow_pass, 1)
    turn(1, [(0, -1), (0, 1)])
    turn(1 + 3, [(-1, -1), (-1, 1)])
    each(slow_near, 2)
    each(slow_pass, 2)
    turn(1 + 1, [(1, -1), (1, 1)])
    each(slow_far, 0)
    turn(1 + 2, [(2, -1), (2, 1)])
    each(slow_far, -1)
    norm_arrive(y, lambda i: norm.at[core, i], 5)
    send(norm.at[core], norm_sent.at[8], norm_came.at[8], {"core": sibling})
    turn(5, [(0, 2)])
    each(slow_far, 1)
    turn(5 + 3, [(-1, 2)])
    each(slow_far, 2)
    turn(5 + 1, [(1, 2)])

    for k in range(2):
        arrive(land.at[k, core, pl.ds(0, 15)], sent.at[k])
        arrive(land.at[k, core], gave.at[k])
    for piece, slots in ((one, (0,)), (pair, (1,)), (line, (2, 3, 4)), (plane, (5, 6, 7)), (norm.at[core], (8,))):
        for slot in slots:
            arrive(piece, norm_sent.at[slot])
    arrive(norm.at[sibling], norm_came.at[8])
    turn(5 + 2, [(2, 2)])


def gather(train_gate, low_gate, high_gate, train_up, low_up, high_up, norm_train, norm_step):
    rows, width = train_gate.shape
    rank = low_gate.shape[1]
    vmem = pl.BlockSpec(memory_space=pltpu.VMEM)
    hbm = pl.BlockSpec(memory_space=pltpu.HBM)
    dma = pltpu.SemaphoreType.DMA
    return pl.pallas_call(
        gather_kernel,
        name="gather",
        out_shape=(
            pltpu.VMEM((2, width, 2 * CHIPS * rows), jnp.bfloat16),
            pltpu.VMEM((2, SIDE, SIDE, SIDE, 1, LANES), jnp.float32),
        ),
        in_specs=[hbm] * 8,
        out_specs=(vmem, vmem),
        scratch_shapes=[
            pltpu.VMEM((2, rows, width), jnp.bfloat16),
            pltpu.VMEM((2, rank, rows), jnp.bfloat16),
            pltpu.VMEM((2, rank, width), jnp.bfloat16),
            pltpu.SMEM((2, 16), jnp.float32),
            pltpu.VMEM((2, 2, CHIPS, rows, width), jnp.bfloat16),
            dma((8,)),
            dma((2,)), dma((2, 22)), dma((2,)), dma((2, 9)), dma((9,)), dma((9,)),
        ],
        compiler_params=pltpu.CompilerParams(
            collective_id=0, has_side_effects=True, vmem_limit_bytes=28 * 2**20
        ),
    )(*(
        pltpu.with_memory_space_constraint(a, pltpu.HBM)
        for a in (train_gate, low_gate.T, high_gate, train_up, low_up.T, high_up, norm_train, norm_step)
    ))


PIECES = 4


def finish_kernel(turned, norm, serve_gate, serve_up, serve_norm, sems):
    rows = serve_gate.shape[0] // PIECES
    copies = [
        pltpu.make_async_copy(turned.at[k, pl.ds(i * rows, rows)], out.at[pl.ds(i * rows, rows)], sems.at[k, i])
        for k, out in enumerate((serve_gate, serve_up))
        for i in range(PIECES)
    ]
    for copy in copies:
        copy.start()
    serve_norm[...] = jnp.sum(norm[...], axis=(0, 3)).reshape(CHIPS, LANES).astype(jnp.bfloat16)
    for copy in copies:
        copy.wait()


def finish(turned, norm):
    vmem = pl.BlockSpec(memory_space=pltpu.VMEM)
    hbm = pl.BlockSpec(memory_space=pl.ANY)
    return pl.pallas_call(
        finish_kernel,
        name="finish",
        out_shape=(
            jax.ShapeDtypeStruct(turned.shape[1:], jnp.bfloat16),
            jax.ShapeDtypeStruct(turned.shape[1:], jnp.bfloat16),
            jax.ShapeDtypeStruct((CHIPS, LANES), jnp.bfloat16),
        ),
        in_specs=[vmem] * 2,
        out_specs=(hbm, hbm, vmem),
        scratch_shapes=[pltpu.SemaphoreType.DMA((2, PIECES))],
        compiler_params=pltpu.CompilerParams(vmem_limit_bytes=4 * 2**20),
    )(turned, norm)


def local(*args):
    serve_gate, serve_up, serve_norm = finish(*gather(*args))
    return serve_gate, serve_up, serve_norm.reshape(-1)


def solution(mesh):
    finer = Mesh(
        mesh.devices.reshape(mesh.shape["trial"], SIDE, SIDE, 2, mesh.shape["cols"]),
        ("trial", "y", "x", "core", "cols"),
    )
    in_specs = (
        P(TRIAL_SHARD, "cols"),
        P(TRIAL_SHARD, None),
        P("trial", "cols"),
        P(TRIAL_SHARD, "cols"),
        P(TRIAL_SHARD, None),
        P("trial", "cols"),
        P(TRIAL_SHARD_COLS),
        P(TRIAL_SHARD_COLS),
    )
    out_specs = (P(("trial", "cols"), None), P(("trial", "cols"), None), P("trial"))
    return jax.shard_map(local, mesh=finer, in_specs=in_specs, out_specs=out_specs, check_vma=False)
```

time: 62.4 us -> 60.3 us (0.966)
  Pallas kernels: 61.7 us -> 59.6 us
    pallas_call x1, Pallas kernels: 54.3 us -> 53.1 us  [gather(): pl.pallas_call(gather_kernel, name='gather', out_shape=(pltpu.VMEM((2, wi...]
    pallas_call x1, Pallas kernels: 7.4 us -> 6.52 us  [finish(): pl.pallas_call(finish_kernel, name='finish', out_shape=(jax.ShapeDtypeStr...]
where the time goes in v3:
time: 60.3 us; the launch traced here: 60.2 us
  Pallas kernels  59.6 us (99%)
  between operations  0.64 us (1%)
    pallas_call x1, Pallas kernels, gather(): pl.pallas_call(gather_kernel, name='gather', out_shape=(pltpu.VMEM((2, wi...  53.1 us
    pallas_call x1, Pallas kernels, finish(): pl.pallas_call(finish_kernel, name='finish', out_shape=(jax.ShapeDtypeStr...  6.52 us

profile of v3, /device:TPU:1, one launch (start us, length us, event | category | flops | bytes accessed | tf_op | source)
XLA Modules:
  0.0 60.2 jit_solution(13601080304236802490)
XLA Ops:
  0.6 53.1 %gather.1 = (bf16[2,2048,2048]{2,1,0:T(8,128)(2,1)S(1)}, f32[2,4,4,4,1,128]{5,4,3,2,1,0:T(1,128)S(1)}) custom-call(bf16[64,2048]{1,0:T(8,128)(2,1)} %train_gate.1, bf16[16,64]{1,0:T(8,128)(2,1)} %bitcast.3, bf16[16,2048]{1,0:T(8,128)(2,1)} %high_gate.1, bf16[64,2048]{1,0:T(8,128)(2,1)} %train_up.1, bf16[16,64]{1,0:T(8,128)(2,1)} %bitcast.4, ...), custom_call_target="tpu_custom_call" | custom-call | tf_op jit(solution)/shard_map/gather/pallas_call | solution.py:210
  53.7 6.5 %finish.1 = (bf16[2048,2048]{1,0:T(8,128)(2,1)}, bf16[2048,2048]{1,0:T(8,128)(2,1)}, bf16[16,128]{1,0:T(8,128)(2,1)}) custom-call(bf16[2,2048,2048]{2,1,0:T(8,128)(2,1)S(1)} %get-tuple-element.8.turned, f32[2,4,4,4,1,128]{5,4,3,2,1,0:T(1,128)S(1)} %get-tuple-element.9.norm), custom_call_target="tpu_custom_call" | custom-call | tf_op jit(solution)/shard_map/finish/pallas_call | solution.py:257

commit v4 on v3

v4 whole, which is shorter than its diff:
```python
import functools

import jax
import jax.numpy as jnp
from jax import lax
from jax.experimental import pallas as pl
from jax.experimental.pallas import tpu as pltpu
from jax.sharding import Mesh
from jax.sharding import PartitionSpec as P

TRIAL_SHARD = ("trial", "y", "x", "core")
TRIAL_SHARD_COLS = ("trial", "y", "x", "core", "cols")
MESH_ID = pl.DeviceIdType.MESH
MIX_RATE = 2.0
SIDE = 4
CHIPS = SIDE * SIDE
LANES = 128


def gather_kernel(
    train_gate, low_gate, high_gate, train_up, low_up, high_up, norm_train, norm_step,
    turned, whole_gain,
    train, low, high, gain, norm, land, loaded, sent, came, gave, took, norm_sent, norm_came,
):
    y, x, core, col = (lax.axis_index(a) for a in ("y", "x", "core", "cols"))
    sibling = 1 - core

    def wrap(i):
        return lax.rem(i + SIDE, SIDE)

    width = train.shape[2]
    half = width // 2
    beside, across = col + 1 - 2 * lax.rem(col, 2), wrap(col + 2)
    barrier = pltpu.get_barrier_semaphore()
    partners = [{"cols": across}, {"cols": beside}]
    partners += [{"x": wrap(x + 1)}, {"x": wrap(x - 1)}, {"y": wrap(y + 1)}, {"y": wrap(y - 1)}, {"core": sibling}]
    for device in partners:
        pl.semaphore_signal(barrier, inc=1, device_id=device, device_id_type=MESH_ID)

    pairs = [
        (train_gate, train.at[0]), (low_gate, low.at[0]), (high_gate, high.at[0]),
        (train_up, train.at[1]), (low_up, low.at[1]), (high_up, high.at[1]),
        (norm_train, gain.at[0]), (norm_step, gain.at[1]),
    ]
    loads = [pltpu.make_async_copy(src, dst, loaded.at[k]) for k, (src, dst) in enumerate(pairs)]
    for load in loads:
        load.start()

    def merge(k):
        for load in loads[3 * k : 3 * k + 3]:
            load.wait()
        product = lax.dot_general(
            low[k], high[k], (((0,), (0,)), ((), ())), preferred_element_type=jnp.float32
        )
        merged = train[k].astype(jnp.float32) + MIX_RATE * product
        land[k, core, y * SIDE + x] = merged.astype(jnp.bfloat16)

    merge(0)
    for load in loads[6:]:
        load.wait()
    lane = lax.broadcasted_iota(jnp.int32, (1, LANES), 1)
    row = jnp.zeros((1, LANES), jnp.float32)
    first = core * 64 + col * 16
    for i in range(16):
        row = jnp.where(lane == first + i, gain[0, i] + gain[1, i], row)
    norm[core, y, x, col] = row
    pl.semaphore_wait(barrier, len(partners))

    def send(piece, sent_sem, came_sem, device):
        pltpu.make_async_remote_copy(
            src_ref=piece, dst_ref=piece, send_sem=sent_sem, recv_sem=came_sem, device_id=device, device_id_type=MESH_ID
        ).start()

    def arrive(piece, sem):
        pltpu.make_async_copy(piece, piece, sem).wait()

    def place(k, f, s):
        at_x, at_y = (x + f, y + s) if k == 0 else (x + s, y + f)
        return wrap(at_y) * SIDE + wrap(at_x)

    def block(k, f, s, at=0, width=width):
        return land.at[k, core, place(k, f, s), :, pl.ds(at, width)]

    def push(k, along_fast, step, piece, slot):
        axis, at = ("x", x) if along_fast == (k == 0) else ("y", y)
        send(piece, sent, came.at[k, slot], {axis: wrap(at + step)})

    def share(piece, group):
        send(piece, gave, took.at[group], {"core": sibling})

    def fast_own(k):
        for step in (1, -1):
            push(k, True, step, block(k, 0, 0), 0)

    def fast_near(k):
        arrive(land.at[k, core, pl.ds(0, 2)], came.at[k, 0])
        push(k, True, 1, block(k, -1, 0, 0, half), 1)
        push(k, True, -1, block(k, 1, 0, half, half), 1)
        for f in (-1, 1):
            share(block(k, f, 0), 0)

    def fast_far(k):
        arrive(land.at[k, core, 0], came.at[k, 1])
        share(block(k, 2, 0), 0)

    def slow_own(k, f):
        for step in (1, -1):
            push(k, False, step, block(k, f, 0), 2 + f % SIDE)

    def slow_near(k, f):
        arrive(land.at[k, core, pl.ds(0, 2)], came.at[k, 2 + f % SIDE])
        for s in (-1, 1):
            share(block(k, f, s), 1 + f % SIDE)

    def slow_pass(k, f, at=0, size=half, slot=None):
        for step, start in ((1, at), (-1, half + at)):
            push(k, False, step, block(k, f, -step, start, size), slot or 6 + f % SIDE)

    def slow_far(k, f):
        arrive(land.at[k, core, 0], came.at[k, 6 + f % SIDE])
        share(block(k, f, 2), 5 + f % SIDE)

    def last_far(k, at, slot, group):
        arrive(land.at[k, core, 0, :, pl.ds(0, half)], came.at[k, slot])
        for start in (at, half + at):
            share(block(k, 2, 2, start, half // 2), group)

    def each(step, *args):
        for k in range(2):
            step(k, *args)

    def turn(group, chips, ranges=None, amount=width):
        arrive(land.at[:, sibling, pl.ds(0, len(chips)), :, pl.ds(0, amount)], took.at[group])
        for k in range(2):
            for f, s in chips:
                chip = place(k, f, s)
                lanes = pl.ds(pl.multiple_of(chip * LANES, LANES), LANES)
                for at, size in ranges or [(0, width)]:
                    tile = [land[k, c, chip, :, pl.ds(at, size)] for c in range(2)]
                    turned[k, pl.ds(at, size), lanes] = jnp.concatenate(tile, axis=0).T

    def norm_send(piece, axis, at, slot):
        for k in (1, 2, 3):
            send(piece, norm_sent.at[slot], norm_came.at[slot], {axis: wrap(at + k)})

    one = norm.at[core, y, x, col]
    pair = norm.at[core, y, x, pl.ds(col - lax.rem(col, 2), 2)]
    other_pair = norm.at[core, y, x, pl.ds(across - lax.rem(across, 2), 2)]
    three_lines, three_planes = norm.at[core, y, pl.ds(0, 3)], norm.at[core, pl.ds(0, 3)]

    fast_own(0)
    slow_own(0, 0)
    send(one, norm_sent.at[0], norm_came.at[0], {"cols": beside})
    merge(1)
    share(block(0, 0, 0), 0)
    arrive(norm.at[core, y, x, beside], norm_came.at[0])
    fast_own(1)
    slow_own(1, 0)
    send(pair, norm_sent.at[1], norm_came.at[1], {"cols": across})
    share(block(1, 0, 0), 0)
    fast_near(0)
    arrive(other_pair, norm_came.at[1])
    norm_send(norm.at[core, y, x], "x", x, 2)
    slow_own(0, -1)
    slow_near(0, 0)
    fast_near(1)
    slow_near(1, 0)
    slow_own(0, 1)
    slow_pass(1, 0)
    slow_own(1, -1)
    slow_own(1, 1)
    fast_far(0)
    slow_own(0, 2)
    slow_pass(0, 0)
    slow_near(0, -1)
    fast_far(1)
    slow_own(1, 2)
    slow_near(1, -1)
    arrive(three_lines, norm_came.at[2])
    norm_send(norm.at[core, y], "y", y, 3)
    each(slow_pass, -1)
    each(slow_near, 1)
    each(slow_pass, 1)
    turn(0, [(0, 0), (-1, 0), (1, 0), (2, 0)])
    each(slow_near, 2)
    each(slow_pass, 2, 0, half // 2)
    each(slow_pass, 2, half // 2, half // 2, 10)
    turn(1, [(0, -1), (0, 1)])
    turn(1 + 3, [(-1, -1), (-1, 1)])
    each(slow_far, 0)
    turn(1 + 1, [(1, -1), (1, 1)])
    each(slow_far, -1)
    turn(1 + 2, [(2, -1), (2, 1)])
    arrive(three_planes, norm_came.at[3])
    send(norm.at[core], norm_sent.at[4], norm_came.at[4], {"core": sibling})
    turn(5, [(0, 2)])
    each(slow_far, 1)
    turn(5 + 3, [(-1, 2)])
    arrive(norm.at[sibling], norm_came.at[4])
    whole_gain[...] = jnp.sum(norm[...], axis=(0, 3)).reshape(CHIPS, LANES).astype(jnp.bfloat16)
    each(last_far, 0, 6 + 2, 5 + 2)
    each(last_far, half // 2, 10, 9)
    turn(5 + 1, [(1, 2)])
    turn(5 + 2, [(2, 2)], [(0, half // 2), (half, half // 2)], half)
    turn(9, [(2, 2)], [(half // 2, half // 2), (3 * half // 2, half // 2)], half)

    arrive(land.at[:, core, pl.ds(0, 15)], sent)
    arrive(land.at[:, core], gave)
    for slot, piece in enumerate((one, pair, three_lines, three_planes, norm.at[core])):
        arrive(piece, norm_sent.at[slot])


def gather(train_gate, low_gate, high_gate, train_up, low_up, high_up, norm_train, norm_step):
    rows, width = train_gate.shape
    rank = low_gate.shape[1]
    vmem = pl.BlockSpec(memory_space=pltpu.VMEM)
    hbm = pl.BlockSpec(memory_space=pltpu.HBM)
    dma = pltpu.SemaphoreType.DMA
    return pl.pallas_call(
        gather_kernel,
        name="gather",
        out_shape=(
            pltpu.VMEM((2, width, 2 * CHIPS * rows), jnp.bfloat16),
            pltpu.VMEM((CHIPS, LANES), jnp.bfloat16),
        ),
        in_specs=[hbm] * 8,
        out_specs=(vmem, vmem),
        scratch_shapes=[
            pltpu.VMEM((2, rows, width), jnp.bfloat16),
            pltpu.VMEM((2, rank, rows), jnp.bfloat16),
            pltpu.VMEM((2, rank, width), jnp.bfloat16),
            pltpu.SMEM((2, 16), jnp.float32),
            pltpu.VMEM((2, SIDE, SIDE, SIDE, 1, LANES), jnp.float32),
            pltpu.VMEM((2, 2, CHIPS, rows, width), jnp.bfloat16),
            dma((8,)), dma, dma((2, 11)), dma, dma((10,)), dma((5,)), dma((5,)),
        ],
        compiler_params=pltpu.CompilerParams(
            collective_id=0, has_side_effects=True, vmem_limit_bytes=28 * 2**20
        ),
    )(*(
        pltpu.with_memory_space_constraint(a, pltpu.HBM)
        for a in (train_gate, low_gate.T, high_gate, train_up, low_up.T, high_up, norm_train, norm_step)
    ))


def finish_kernel(turned, gain, serve_gate, serve_up, serve_norm, sems):
    rows = serve_gate.shape[0] // 2
    halves = [pl.ds(i * rows, rows) for i in range(2)]
    pairs = [(turned.at[k, h], out.at[h]) for k, out in enumerate((serve_gate, serve_up)) for h in halves]
    pairs.append((gain, serve_norm))
    copies = [pltpu.make_async_copy(src, dst, sems.at[k]) for k, (src, dst) in enumerate(pairs)]
    for copy in copies:
        copy.start()
    for copy in copies:
        copy.wait()


def finish(turned, gain):
    vmem = pl.BlockSpec(memory_space=pltpu.VMEM)
    hbm = pl.BlockSpec(memory_space=pl.ANY)
    return pl.pallas_call(
        finish_kernel,
        name="finish",
        out_shape=(
            jax.ShapeDtypeStruct(turned.shape[1:], jnp.bfloat16),
            jax.ShapeDtypeStruct(turned.shape[1:], jnp.bfloat16),
            jax.ShapeDtypeStruct(gain.shape, jnp.bfloat16),
        ),
        in_specs=[vmem] * 2,
        out_specs=(hbm, hbm, hbm),
        scratch_shapes=[pltpu.SemaphoreType.DMA((5,))],
        compiler_params=pltpu.CompilerParams(vmem_limit_bytes=4 * 2**20),
    )(turned, gain)


def local(*args):
    serve_gate, serve_up, serve_norm = finish(*gather(*args))
    return serve_gate, serve_up, serve_norm.reshape(-1)


def solution(mesh):
    finer = Mesh(
        mesh.devices.reshape(mesh.shape["trial"], SIDE, SIDE, 2, mesh.shape["cols"]),
        ("trial", "y", "x", "core", "cols"),
    )
    in_specs = (
        P(TRIAL_SHARD, "cols"),
        P(TRIAL_SHARD, None),
        P("trial", "cols"),
        P(TRIAL_SHARD, "cols"),
        P(TRIAL_SHARD, None),
        P("trial", "cols"),
        P(TRIAL_SHARD_COLS),
        P(TRIAL_SHARD_COLS),
    )
    out_specs = (P(("trial", "cols"), None), P(("trial", "cols"), None), P("trial"))
    return jax.shard_map(local, mesh=finer, in_specs=in_specs, out_specs=out_specs, check_vma=False)
```

time: 60.3 us -> 59.3 us (0.983)
  Pallas kernels: 59.6 us -> 58.5 us
where the time goes in v4:
time: 59.3 us; the launch traced here: 59.2 us
  Pallas kernels  58.5 us (99%)
  between operations  0.64 us (1%)
    pallas_call x1, Pallas kernels, gather(): pl.pallas_call(gather_kernel, name='gather', out_shape=(pltpu.VMEM((2, wi...  52.6 us
    pallas_call x1, Pallas kernels, finish(): pl.pallas_call(finish_kernel, name='finish', out_shape=(jax.ShapeDtypeStr...  5.96 us

profile of v4, /device:TPU:1, one launch (start us, length us, event | category | flops | bytes accessed | tf_op | source)
XLA Modules:
  0.0 59.2 jit_solution(15942287698261283502)
XLA Ops:
  0.6 52.6 %gather.1 = (bf16[2,2048,2048]{2,1,0:T(8,128)(2,1)S(1)}, bf16[16,128]{1,0:T(8,128)(2,1)S(1)}) custom-call(bf16[64,2048]{1,0:T(8,128)(2,1)} %train_gate.1, bf16[16,64]{1,0:T(8,128)(2,1)} %bitcast.3, bf16[16,2048]{1,0:T(8,128)(2,1)} %high_gate.1, bf16[64,2048]{1,0:T(8,128)(2,1)} %train_up.1, bf16[16,64]{1,0:T(8,128)(2,1)} %bitcast.4, ...), custom_call_target="tpu_custom_call" | custom-call | tf_op jit(solution)/shard_map/gather/pallas_call | solution.py:219
  53.2 6.0 %finish.1 = (bf16[2048,2048]{1,0:T(8,128)(2,1)}, bf16[2048,2048]{1,0:T(8,128)(2,1)}, bf16[16,128]{1,0:T(8,128)(2,1)}) custom-call(bf16[2,2048,2048]{2,1,0:T(8,128)(2,1)S(1)} %get-tuple-element.8.turned, bf16[16,128]{1,0:T(8,128)(2,1)S(1)} %get-tuple-element.9.gain), custom_call_target="tpu_custom_call" | custom-call | tf_op jit(solution)/shard_map/finish/pallas_call | solution.py:261

commit v5 on v4

v5 whole, which is shorter than its diff:
```python
import functools

import jax
import jax.numpy as jnp
from jax import lax
from jax.experimental import pallas as pl
from jax.experimental.pallas import tpu as pltpu
from jax.sharding import Mesh
from jax.sharding import PartitionSpec as P

TRIAL_SHARD = ("trial", "y", "x", "core")
TRIAL_SHARD_COLS = ("trial", "y", "x", "core", "cols")
MESH_ID = pl.DeviceIdType.MESH
MIX_RATE = 2.0
SIDE = 4
CHIPS = SIDE * SIDE
LANES = 128


def gather_kernel(
    train_gate, low_gate, high_gate, train_up, low_up, high_up, norm_train, norm_step,
    turned, whole_gain,
    train, low, high, gain, norm, land, loaded, sent, came, gave, took, norm_came,
):
    y, x, core, col = (lax.axis_index(a) for a in ("y", "x", "core", "cols"))
    sibling = 1 - core
    width = train.shape[2]
    half, quarter, tail = width // 2, width // 4, width // 8

    def wrap(i):
        return lax.rem(i + SIDE, SIDE)

    pairs = [
        (train_gate, train.at[0]), (high_gate, high.at[0]), (low_gate, low.at[0]),
        (train_up, train.at[1]), (high_up, high.at[1]), (low_up, low.at[1]),
        (norm_train, gain.at[0]), (norm_step, gain.at[1]),
    ]
    loads = [pltpu.make_async_copy(src, dst, loaded.at[k]) for k, (src, dst) in enumerate(pairs)]
    for load in loads[:3]:
        load.start()

    beside, across = col + 1 - 2 * lax.rem(col, 2), wrap(col + 2)
    barrier = pltpu.get_barrier_semaphore()
    partners = [{"cols": across}, {"x": wrap(x + 1)}, {"x": wrap(x - 1)}, {"y": wrap(y + 1)}, {"y": wrap(y - 1)}]
    partners += [{"cols": beside}, {"core": sibling}]
    for device in partners:
        pl.semaphore_signal(barrier, inc=1, device_id=device, device_id_type=MESH_ID)
    for load in loads[3:]:
        load.start()

    def send(piece, sent_sem, came_sem, device):
        pltpu.make_async_remote_copy(
            src_ref=piece, dst_ref=piece, send_sem=sent_sem, recv_sem=came_sem, device_id=device, device_id_type=MESH_ID
        ).start()

    def arrive(piece, sem):
        pltpu.make_async_copy(piece, piece, sem).wait()

    def merge(k, at, size):
        product = lax.dot_general(
            low[k], high[k, :, pl.ds(at, size)], (((0,), (0,)), ((), ())), preferred_element_type=jnp.float32
        )
        merged = train[k, :, pl.ds(at, size)].astype(jnp.float32) + MIX_RATE * product
        land[k, core, y * SIDE + x, :, pl.ds(at, size)] = merged.astype(jnp.bfloat16)

    def place(k, f, s):
        at_x, at_y = (x + f, y + s) if k == 0 else (x + s, y + f)
        return wrap(at_y) * SIDE + wrap(at_x)

    def block(k, f, s, at=0, size=width, side=core):
        return land.at[k, side, place(k, f, s), :, pl.ds(at, size)]

    def push(k, along_fast, step, piece, slot, kind=0):
        axis, at = ("x", x) if along_fast == (k == 0) else ("y", y)
        send(piece, sent.at[kind], came.at[slot], {axis: wrap(at + step)})

    def share(piece, group, kind=0):
        send(piece, gave.at[kind], took.at[group], {"core": sibling})

    def own(k, at=0, size=width):
        for along_fast, slot in ((True, 6 * k), (False, 6 * k + 2)):
            for step in (1, -1):
                push(k, along_fast, step, block(k, 0, 0, at, size), slot)

    def fast_near(k):
        arrive(land.at[k, core, pl.ds(0, 2)], came.at[6 * k])
        push(k, True, 1, block(k, -1, 0, 0, half), 6 * k + 1)
        push(k, True, -1, block(k, 1, 0, half, half), 6 * k + 1)
        for f in (-1, 1):
            share(block(k, f, 0), 0)

    def fast_far(k):
        arrive(land.at[k, core, 0], came.at[6 * k + 1])
        share(block(k, 2, 0), 0)

    def slow_own(k, f):
        for step in (1, -1):
            push(k, False, step, block(k, f, 0), 6 * k + 2 + f % SIDE)

    def slow_near(k, f):
        arrive(land.at[k, core, pl.ds(0, 2)], came.at[6 * k + 2 + f % SIDE])
        for s in (-1, 1):
            share(block(k, f, s), {0: 0, -1: 0, 1: 1, 2: 2}[f])

    def slow_pass(k, f, slot, at=0, size=half, side=core):
        for step, start in ((1, at), (-1, half + at)):
            push(k, False, step, block(k, f, -step, start, size, side), slot, int(f == 0))

    def slow_far(slot, count, size, pieces, group, kind=0):
        arrive(land.at[:, core, pl.ds(0, count), :, pl.ds(0, size)], came.at[slot])
        for k in range(2):
            for f, starts, length, side in pieces:
                for start in starts:
                    share(block(k, f, 2, start, length, side), group, int(f == 0))

    def theirs(group, blocks, size=width):
        arrive(land.at[:, sibling, pl.ds(0, blocks), :, pl.ds(0, size)], took.at[group])

    def turn(chips, ranges=((0, width),)):
        for k in range(2):
            for f, s in chips:
                chip = place(k, f, s)
                lanes = pl.ds(pl.multiple_of(chip * LANES, LANES), LANES)
                for at, size in ranges:
                    tile = [land[k, c, chip, :, pl.ds(at, size)] for c in range(2)]
                    turned[k, pl.ds(at, size), lanes] = jnp.concatenate(tile, axis=0).T

    def norm_send(pieces, slot):
        for piece, device in pieces:
            send(piece, loaded.at[slot], norm_came.at[slot], device)

    one = norm.at[core, y, x, col]
    pair = norm.at[core, y, x, pl.ds(col - lax.rem(col, 2), 2)]
    other_pair = norm.at[core, y, x, pl.ds(across - lax.rem(across, 2), 2)]
    three_lines, three_planes = norm.at[core, y, pl.ds(0, 3)], norm.at[core, pl.ds(0, 3)]

    for load in loads[:3]:
        load.wait()
    merge(0, 0, half)
    pl.semaphore_wait(barrier, len(partners))
    own(0, 0, half)
    merge(0, half, half)
    own(0, half, half)

    for load in loads[3:]:
        load.wait()
    lane = lax.broadcasted_iota(jnp.int32, (1, LANES), 1)
    row = jnp.zeros((1, LANES), jnp.float32)
    first = core * 64 + col * 16
    for i in range(16):
        row = jnp.where(lane == first + i, gain[0, i] + gain[1, i], row)
    norm[core, y, x, col] = row
    merge(1, 0, width)
    norm_send([(one, {"cols": beside})], 0)
    own(1)
    for k in range(2):
        share(block(k, 0, 0), 0)
    arrive(norm.at[core, y, x, beside], norm_came.at[0])
    norm_send([(pair, {"cols": across})], 1)

    firsts, seconds = (0, half), (quarter, half + quarter)
    first_ranges, second_ranges = [[(at, quarter) for at in starts] for starts in (firsts, seconds)]
    last = (half - tail, width - tail)

    fast_near(0)
    arrive(other_pair, norm_came.at[1])
    norm_send([(norm.at[core, y, x], {"x": wrap(x + i)}) for i in (1, 2, 3)], 2)
    slow_own(0, -1)
    slow_near(0, 0)
    fast_near(1)
    slow_near(1, 0)
    slow_own(0, 1)
    slow_pass(1, 0, 12, 0, quarter)
    slow_own(1, -1)
    slow_own(1, 1)
    fast_far(0)
    slow_own(0, 2)
    slow_pass(0, 0, 12, 0, quarter)
    slow_near(0, -1)
    fast_far(1)
    slow_own(1, 2)
    slow_near(1, -1)
    arrive(three_lines, norm_came.at[2])
    norm_send([(norm.at[core, y], {"y": wrap(y + i)}) for i in (1, 2, 3)], 3)
    for k in range(2):
        slow_pass(k, -1, 12)
    for k in range(2):
        slow_near(k, 1)
        slow_pass(k, 1, 14)
    theirs(0, 8)

    @pl.when(core == 1)
    def _():
        for k in range(2):
            slow_pass(k, 0, 13, quarter, quarter)
            slow_pass(k, 0, 13, quarter, quarter, sibling)

    turn([(0, 0), (-1, 0), (1, 0), (2, 0)])
    slow_near(0, 2)
    slow_pass(0, 2, 15, 0, half - tail)
    slow_pass(0, 2, 16, half - tail, tail)
    turn([(0, -1), (0, 1)])
    slow_near(1, 2)
    slow_pass(1, 2, 15, 0, half - tail)
    slow_pass(1, 2, 16, half - tail, tail)
    turn([(-1, -1), (-1, 1)])
    theirs(1, 2)
    slow_far(12, 3, half, [(-1, (0,), width, core), (0, firsts, quarter, core)], 3)
    turn([(1, -1), (1, 1)])
    arrive(three_planes, norm_came.at[3])
    norm_send([(norm.at[core], {"core": sibling})], 4)

    theirs(2, 2)
    turn([(2, -1), (2, 1)])
    slow_far(14, 1, width, [(1, (0,), width, core)], 4)

    @pl.when(core == 1)
    def _():
        slow_far(13, 1, width, [(0, seconds, quarter, core), (0, seconds, quarter, sibling)], 6)

    slow_far(15, 1, width - 2 * tail, [(2, firsts, half - tail, core)], 5)
    theirs(3, 3, half)
    turn([(-1, 2)])
    turn([(0, 2)], first_ranges)
    slow_far(16, 1, 2 * tail, [(2, last, tail, core)], 7)
    arrive(norm.at[sibling], norm_came.at[4])
    whole_gain[...] = jnp.sum(norm[...], axis=(0, 3)).reshape(CHIPS, LANES).astype(jnp.bfloat16)

    @pl.when(core == 1)
    def _():
        arrive(land.at[:, core, pl.ds(0, 3), :, pl.ds(0, half)], sent.at[1])
        arrive(land.at[:, core, pl.ds(0, 3), :, pl.ds(0, half)], gave.at[1])

    @pl.when(core == 0)
    def _():
        arrive(land.at[:, core, pl.ds(0, 1), :, pl.ds(0, half)], sent.at[1])
        arrive(land.at[:, core, pl.ds(0, 1), :, pl.ds(0, half)], gave.at[1])
        theirs(6, 1)

    turn([(0, 2)], second_ranges)
    theirs(4, 1)
    turn([(1, 2)])
    theirs(5, 1, width - 2 * tail)
    turn([(2, 2)], [(at, half - tail) for at in firsts])
    theirs(7, 1, 2 * tail)
    turn([(2, 2)], [(at, tail) for at in last])
    arrive(land.at[:, core, pl.ds(0, 14)], sent.at[0])
    arrive(land.at[:, core, pl.ds(0, 15)], gave.at[0])
    for slot, piece in enumerate((one, pair, three_lines, three_planes, norm.at[core])):
        arrive(piece, loaded.at[slot])


def gather(train_gate, low_gate, high_gate, train_up, low_up, high_up, norm_train, norm_step):
    rows, width = train_gate.shape
    rank = low_gate.shape[1]
    vmem = pl.BlockSpec(memory_space=pltpu.VMEM)
    hbm = pl.BlockSpec(memory_space=pltpu.HBM)
    dma = pltpu.SemaphoreType.DMA
    return pl.pallas_call(
        gather_kernel,
        name="gather",
        out_shape=(
            pltpu.VMEM((2, width, 2 * CHIPS * rows), jnp.bfloat16),
            pltpu.VMEM((CHIPS, LANES), jnp.bfloat16),
        ),
        in_specs=[hbm] * 8,
        out_specs=(vmem, vmem),
        scratch_shapes=[
            pltpu.VMEM((2, rows, width), jnp.bfloat16),
            pltpu.VMEM((2, rank, rows), jnp.bfloat16),
            pltpu.VMEM((2, rank, width), jnp.bfloat16),
            pltpu.SMEM((2, 16), jnp.float32),
            pltpu.VMEM((2, SIDE, SIDE, SIDE, 1, LANES), jnp.float32),
            pltpu.VMEM((2, 2, CHIPS, rows, width), jnp.bfloat16),
            dma((8,)), dma((2,)), dma((17,)), dma((2,)), dma((8,)), dma((5,)),
        ],
        compiler_params=pltpu.CompilerParams(
            collective_id=0, has_side_effects=True, vmem_limit_bytes=28 * 2**20
        ),
    )(*(
        pltpu.with_memory_space_constraint(a, pltpu.HBM)
        for a in (train_gate, low_gate.T, high_gate, train_up, low_up.T, high_up, norm_train, norm_step)
    ))


def finish_kernel(turned, gain, serve_gate, serve_up, serve_norm, sems):
    rows = serve_gate.shape[0] // 2
    halves = [pl.ds(i * rows, rows) for i in range(2)]
    pairs = [(turned.at[k, h], out.at[h]) for k, out in enumerate((serve_gate, serve_up)) for h in halves]
    pairs.append((gain, serve_norm))
    copies = [pltpu.make_async_copy(src, dst, sems.at[k]) for k, (src, dst) in enumerate(pairs)]
    for copy in copies:
        copy.start()
    for copy in copies:
        copy.wait()


def finish(turned, gain):
    vmem = pl.BlockSpec(memory_space=pltpu.VMEM)
    hbm = pl.BlockSpec(memory_space=pl.ANY)
    return pl.pallas_call(
        finish_kernel,
        name="finish",
        out_shape=(
            jax.ShapeDtypeStruct(turned.shape[1:], jnp.bfloat16),
            jax.ShapeDtypeStruct(turned.shape[1:], jnp.bfloat16),
            jax.ShapeDtypeStruct(gain.shape, jnp.bfloat16),
        ),
        in_specs=[vmem] * 2,
        out_specs=(hbm, hbm, hbm),
        scratch_shapes=[pltpu.SemaphoreType.DMA((5,))],
        compiler_params=pltpu.CompilerParams(vmem_limit_bytes=4 * 2**20),
    )(turned, gain)


def local(*args):
    serve_gate, serve_up, serve_norm = finish(*gather(*args))
    return serve_gate, serve_up, serve_norm.reshape(-1)


def solution(mesh):
    finer = Mesh(
        mesh.devices.reshape(mesh.shape["trial"], SIDE, SIDE, 2, mesh.shape["cols"]),
        ("trial", "y", "x", "core", "cols"),
    )
    in_specs = (
        P(TRIAL_SHARD, "cols"),
        P(TRIAL_SHARD, None),
        P("trial", "cols"),
        P(TRIAL_SHARD, "cols"),
        P(TRIAL_SHARD, None),
        P("trial", "cols"),
        P(TRIAL_SHARD_COLS),
        P(TRIAL_SHARD_COLS),
    )
    out_specs = (P(("trial", "cols"), None), P(("trial", "cols"), None), P("trial"))
    return jax.shard_map(local, mesh=finer, in_specs=in_specs, out_specs=out_specs, check_vma=False)
```

time: 59.3 us -> 58.7 us (0.990)
  no operation moved by 1% of the time
where the time goes in v5:
time: 58.7 us; the launch traced here: 58.6 us
  Pallas kernels  58 us (99%)
  between operations  0.64 us (1%)
    pallas_call x1, Pallas kernels, gather(): pl.pallas_call(gather_kernel, name='gather', out_shape=(pltpu.VMEM((2, wi...  52 us
    pallas_call x1, Pallas kernels, finish(): pl.pallas_call(finish_kernel, name='finish', out_shape=(jax.ShapeDtypeStr...  5.96 us

profile of v5, /device:TPU:1, one launch (start us, length us, event | category | flops | bytes accessed | tf_op | source)
XLA Modules:
  0.0 58.6 jit_solution(13439731187795462390)
XLA Ops:
  0.6 52.0 %gather.1 = (bf16[2,2048,2048]{2,1,0:T(8,128)(2,1)S(1)}, bf16[16,128]{1,0:T(8,128)(2,1)S(1)}) custom-call(bf16[64,2048]{1,0:T(8,128)(2,1)} %train_gate.1, bf16[16,64]{1,0:T(8,128)(2,1)} %bitcast.3, bf16[16,2048]{1,0:T(8,128)(2,1)} %high_gate.1, bf16[64,2048]{1,0:T(8,128)(2,1)} %train_up.1, bf16[16,64]{1,0:T(8,128)(2,1)} %bitcast.4, ...), custom_call_target="tpu_custom_call" | custom-call | tf_op jit(solution)/shard_map/gather/pallas_call | solution.py:259
  52.7 6.0 %finish.1 = (bf16[2048,2048]{1,0:T(8,128)(2,1)}, bf16[2048,2048]{1,0:T(8,128)(2,1)}, bf16[16,128]{1,0:T(8,128)(2,1)}) custom-call(bf16[2,2048,2048]{2,1,0:T(8,128)(2,1)S(1)} %get-tuple-element.8.turned, bf16[16,128]{1,0:T(8,128)(2,1)S(1)} %get-tuple-element.9.gain), custom_call_target="tpu_custom_call" | custom-call | tf_op jit(solution)/shard_map/finish/pallas_call | solution.py:301

commit v6 on v5

--- a/solution.py
+++ b/solution.py
@@ -112,6 +112,11 @@
             for f, starts, length, side in pieces:
                 for start in starts:
                     share(block(k, f, 2, start, length, side), group, int(f == 0))
+
+    def last_far(k, slot, starts, size, group):
+        arrive(land.at[k, core, 0, :, pl.ds(0, 2 * size)], came.at[slot + k])
+        for start in starts:
+            share(block(k, 2, 2, start, size), group)
 
     def theirs(group, blocks, size=width):
         arrive(land.at[:, sibling, pl.ds(0, blocks), :, pl.ds(0, size)], took.at[group])
@@ -198,11 +203,11 @@
     turn([(0, 0), (-1, 0), (1, 0), (2, 0)])
     slow_near(0, 2)
     slow_pass(0, 2, 15, 0, half - tail)
-    slow_pass(0, 2, 16, half - tail, tail)
+    slow_pass(0, 2, 17, half - tail, tail)
     turn([(0, -1), (0, 1)])
     slow_near(1, 2)
-    slow_pass(1, 2, 15, 0, half - tail)
-    slow_pass(1, 2, 16, half - tail, tail)
+    slow_pass(1, 2, 16, 0, half - tail)
+    slow_pass(1, 2, 18, half - tail, tail)
     turn([(-1, -1), (-1, 1)])
     theirs(1, 2)
     slow_far(12, 3, half, [(-1, (0,), width, core), (0, firsts, quarter, core)], 3)
@@ -218,13 +223,25 @@
     def _():
         slow_far(13, 1, width, [(0, seconds, quarter, core), (0, seconds, quarter, sibling)], 6)
 
-    slow_far(15, 1, width - 2 * tail, [(2, firsts, half - tail, core)], 5)
     theirs(3, 3, half)
     turn([(-1, 2)])
     turn([(0, 2)], first_ranges)
-    slow_far(16, 1, 2 * tail, [(2, last, tail, core)], 7)
     arrive(norm.at[sibling], norm_came.at[4])
     whole_gain[...] = jnp.sum(norm[...], axis=(0, 3)).reshape(CHIPS, LANES).astype(jnp.bfloat16)
+    for k in range(2):
+        last_far(k, 15, firsts, half - tail, 5)
+    theirs(4, 1)
+    turn([(1, 2)])
+    for k in range(2):
+        last_far(k, 17, last, tail, 7)
+
+    @pl.when(core == 0)
+    def _():
+        theirs(6, 1)
+
+    turn([(0, 2)], second_ranges)
+    theirs(5, 1, width - 2 * tail)
+    turn([(2, 2)], [(at, half - tail) for at in firsts])
 
     @pl.when(core == 1)
     def _():
@@ -235,13 +252,7 @@
     def _():
         arrive(land.at[:, core, pl.ds(0, 1), :, pl.ds(0, half)], sent.at[1])
         arrive(land.at[:, core, pl.ds(0, 1), :, pl.ds(0, half)], gave.at[1])
-        theirs(6, 1)
-
-    turn([(0, 2)], second_ranges)
-    theirs(4, 1)
-    turn([(1, 2)])
-    theirs(5, 1, width - 2 * tail)
-    turn([(2, 2)], [(at, half - tail) for at in firsts])
+
     theirs(7, 1, 2 * tail)
     turn([(2, 2)], [(at, tail) for at in last])
     arrive(land.at[:, core, pl.ds(0, 14)], sent.at[0])
@@ -272,7 +283,7 @@
             pltpu.SMEM((2, 16), jnp.float32),
             pltpu.VMEM((2, SIDE, SIDE, SIDE, 1, LANES), jnp.float32),
             pltpu.VMEM((2, 2, CHIPS, rows, width), jnp.bfloat16),
-            dma((8,)), dma((2,)), dma((17,)), dma((2,)), dma((8,)), dma((5,)),
+            dma((8,)), dma((2,)), dma((19,)), dma((2,)), dma((8,)), dma((5,)),
         ],
         compiler_params=pltpu.CompilerParams(
             collective_id=0, has_side_effects=True, vmem_limit_bytes=28 * 2**20

time: 58.7 us -> 58.8 us (level)
  no operation moved by 1% of the time
where the time goes in v6:
time: 58.8 us; the launch traced here: 58.7 us
  Pallas kernels  58 us (99%)
  between operations  0.64 us (1%)
    pallas_call x1, Pallas kernels, gather(): pl.pallas_call(gather_kernel, name='gather', out_shape=(pltpu.VMEM((2, wi...  52.1 us
    pallas_call x1, Pallas kernels, finish(): pl.pallas_call(finish_kernel, name='finish', out_shape=(jax.ShapeDtypeStr...  5.96 us

profile of v6, /device:TPU:1, one launch (start us, length us, event | category | flops | bytes accessed | tf_op | source)
XLA Modules:
  0.0 58.7 jit_solution(3946790200524654267)
XLA Ops:
  0.6 52.1 %gather.1 = (bf16[2,2048,2048]{2,1,0:T(8,128)(2,1)S(1)}, bf16[16,128]{1,0:T(8,128)(2,1)S(1)}) custom-call(bf16[64,2048]{1,0:T(8,128)(2,1)} %train_gate.1, bf16[16,64]{1,0:T(8,128)(2,1)} %bitcast.3, bf16[16,2048]{1,0:T(8,128)(2,1)} %high_gate.1, bf16[64,2048]{1,0:T(8,128)(2,1)} %train_up.1, bf16[16,64]{1,0:T(8,128)(2,1)} %bitcast.4, ...), custom_call_target="tpu_custom_call" | custom-call | tf_op jit(solution)/shard_map/gather/pallas_call | solution.py:270
  52.7 6.0 %finish.1 = (bf16[2048,2048]{1,0:T(8,128)(2,1)}, bf16[2048,2048]{1,0:T(8,128)(2,1)}, bf16[16,128]{1,0:T(8,128)(2,1)}) custom-call(bf16[2,2048,2048]{2,1,0:T(8,128)(2,1)S(1)} %get-tuple-element.8.turned, bf16[16,128]{1,0:T(8,128)(2,1)S(1)} %get-tuple-element.9.gain), custom_call_target="tpu_custom_call" | custom-call | tf_op jit(solution)/shard_map/finish/pallas_call | solution.py:312

commit v7 on v6

--- a/solution.py
+++ b/solution.py
@@ -20,7 +20,7 @@
 def gather_kernel(
     train_gate, low_gate, high_gate, train_up, low_up, high_up, norm_train, norm_step,
     turned, whole_gain,
-    train, low, high, gain, norm, land, loaded, sent, came, gave, took, norm_came,
+    train, low, high, gain, rows, norm, land, loaded, sent, came, gave, took, norm_came,
 ):
     y, x, core, col = (lax.axis_index(a) for a in ("y", "x", "core", "cols"))
     sibling = 1 - core
@@ -134,9 +134,9 @@
         for piece, device in pieces:
             send(piece, loaded.at[slot], norm_came.at[slot], device)
 
-    one = norm.at[core, y, x, col]
-    pair = norm.at[core, y, x, pl.ds(col - lax.rem(col, 2), 2)]
-    other_pair = norm.at[core, y, x, pl.ds(across - lax.rem(across, 2), 2)]
+    one = rows.at[col]
+    pair = rows.at[pl.ds(col - lax.rem(col, 2), 2)]
+    other_pair = rows.at[pl.ds(across - lax.rem(across, 2), 2)]
     three_lines, three_planes = norm.at[core, y, pl.ds(0, 3)], norm.at[core, pl.ds(0, 3)]
 
     for load in loads[:3]:
@@ -154,13 +154,13 @@
     first = core * 64 + col * 16
     for i in range(16):
         row = jnp.where(lane == first + i, gain[0, i] + gain[1, i], row)
-    norm[core, y, x, col] = row
+    rows[col] = row
     merge(1, 0, width)
     norm_send([(one, {"cols": beside})], 0)
     own(1)
     for k in range(2):
         share(block(k, 0, 0), 0)
-    arrive(norm.at[core, y, x, beside], norm_came.at[0])
+    arrive(rows.at[beside], norm_came.at[0])
     norm_send([(pair, {"cols": across})], 1)
 
     firsts, seconds = (0, half), (quarter, half + quarter)
@@ -169,8 +169,9 @@
 
     fast_near(0)
     arrive(other_pair, norm_came.at[1])
+    norm[core, y, x] = jnp.sum(rows[...], axis=0)
+    slow_own(0, -1)
     norm_send([(norm.at[core, y, x], {"x": wrap(x + i)}) for i in (1, 2, 3)], 2)
-    slow_own(0, -1)
     slow_near(0, 0)
     fast_near(1)
     slow_near(1, 0)
@@ -227,7 +228,7 @@
     turn([(-1, 2)])
     turn([(0, 2)], first_ranges)
     arrive(norm.at[sibling], norm_came.at[4])
-    whole_gain[...] = jnp.sum(norm[...], axis=(0, 3)).reshape(CHIPS, LANES).astype(jnp.bfloat16)
+    whole_gain[...] = jnp.sum(norm[...], axis=0).reshape(CHIPS, LANES).astype(jnp.bfloat16)
     for k in range(2):
         last_far(k, 15, firsts, half - tail, 5)
     theirs(4, 1)
@@ -281,7 +282,8 @@
             pltpu.VMEM((2, rank, rows), jnp.bfloat16),
             pltpu.VMEM((2, rank, width), jnp.bfloat16),
             pltpu.SMEM((2, 16), jnp.float32),
-            pltpu.VMEM((2, SIDE, SIDE, SIDE, 1, LANES), jnp.float32),
+            pltpu.VMEM((SIDE, 1, LANES), jnp.float32),
+            pltpu.VMEM((2, SIDE, SIDE, 1, LANES), jnp.float32),
             pltpu.VMEM((2, 2, CHIPS, rows, width), jnp.bfloat16),
             dma((8,)), dma((2,)), dma((19,)), dma((2,)), dma((8,)), dma((5,)),
         ],

time: 58.8 us -> 58.7 us (level)
  no operation moved by 1% of the time
where the time goes in v7:
time: 58.7 us; the launch traced here: 58.6 us
  Pallas kernels  58 us (99%)
  between operations  0.64 us (1%)
    pallas_call x1, Pallas kernels, gather(): pl.pallas_call(gather_kernel, name='gather', out_shape=(pltpu.VMEM((2, wi...  52 us
    pallas_call x1, Pallas kernels, finish(): pl.pallas_call(finish_kernel, name='finish', out_shape=(jax.ShapeDtypeStr...  5.96 us

profile of v7, /device:TPU:1, one launch (start us, length us, event | category | flops | bytes accessed | tf_op | source)
XLA Modules:
  0.0 58.6 jit_solution(9162515583474385021)
XLA Ops:
  0.6 52.0 %gather.1 = (bf16[2,2048,2048]{2,1,0:T(8,128)(2,1)S(1)}, bf16[16,128]{1,0:T(8,128)(2,1)S(1)}) custom-call(bf16[64,2048]{1,0:T(8,128)(2,1)} %train_gate.1, bf16[16,64]{1,0:T(8,128)(2,1)} %bitcast.3, bf16[16,2048]{1,0:T(8,128)(2,1)} %high_gate.1, bf16[64,2048]{1,0:T(8,128)(2,1)} %train_up.1, bf16[16,64]{1,0:T(8,128)(2,1)} %bitcast.4, ...), custom_call_target="tpu_custom_call" | custom-call | tf_op jit(solution)/shard_map/gather/pallas_call | solution.py:271
  52.7 6.0 %finish.1 = (bf16[2048,2048]{1,0:T(8,128)(2,1)}, bf16[2048,2048]{1,0:T(8,128)(2,1)}, bf16[16,128]{1,0:T(8,128)(2,1)}) custom-call(bf16[2,2048,2048]{2,1,0:T(8,128)(2,1)S(1)} %get-tuple-element.8.turned, bf16[16,128]{1,0:T(8,128)(2,1)S(1)} %get-tuple-element.9.gain), custom_call_target="tpu_custom_call" | custom-call | tf_op jit(solution)/shard_map/finish/pallas_call | solution.py:314

commit v8 on v7

--- a/solution.py
+++ b/solution.py
@@ -35,17 +35,19 @@
         (train_up, train.at[1]), (high_up, high.at[1]), (low_up, low.at[1]),
         (norm_train, gain.at[0]), (norm_step, gain.at[1]),
     ]
-    loads = [pltpu.make_async_copy(src, dst, loaded.at[k]) for k, (src, dst) in enumerate(pairs)]
-    for load in loads[:3]:
-        load.start()
-
+    slots = (0, 1, 2, 0, 1, 2, 3, 4)
+    loads = [pltpu.make_async_copy(src, dst, loaded.at[slot]) for slot, (src, dst) in zip(slots, pairs)]
     beside, across = col + 1 - 2 * lax.rem(col, 2), wrap(col + 2)
     barrier = pltpu.get_barrier_semaphore()
     partners = [{"cols": across}, {"x": wrap(x + 1)}, {"x": wrap(x - 1)}, {"y": wrap(y + 1)}, {"y": wrap(y - 1)}]
     partners += [{"cols": beside}, {"core": sibling}]
-    for device in partners:
+    for device in partners[:5]:
         pl.semaphore_signal(barrier, inc=1, device_id=device, device_id_type=MESH_ID)
-    for load in loads[3:]:
+    for load in loads[:3]:
+        load.start()
+    for device in partners[5:]:
+        pl.semaphore_signal(barrier, inc=1, device_id=device, device_id_type=MESH_ID)
+    for load in loads[6:]:
         load.start()
 
     def send(piece, sent_sem, came_sem, device):
@@ -141,13 +143,15 @@
 
     for load in loads[:3]:
         load.wait()
-    merge(0, 0, half)
+    merge(0, 0, quarter)
     pl.semaphore_wait(barrier, len(partners))
-    own(0, 0, half)
-    merge(0, half, half)
-    own(0, half, half)
-
-    for load in loads[3:]:
+    own(0, 0, quarter)
+    for load in loads[3:6]:
+        load.start()
+    merge(0, quarter, width - quarter)
+    own(0, quarter, width - quarter)
+
+    for load in loads[6:]:
         load.wait()
     lane = lax.broadcasted_iota(jnp.int32, (1, LANES), 1)
     row = jnp.zeros((1, LANES), jnp.float32)
@@ -155,6 +159,8 @@
     for i in range(16):
         row = jnp.where(lane == first + i, gain[0, i] + gain[1, i], row)
     rows[col] = row
+    for load in loads[3:6]:
+        load.wait()
     merge(1, 0, width)
     norm_send([(one, {"cols": beside})], 0)
     own(1)
@@ -285,7 +291,7 @@
             pltpu.VMEM((SIDE, 1, LANES), jnp.float32),
             pltpu.VMEM((2, SIDE, SIDE, 1, LANES), jnp.float32),
             pltpu.VMEM((2, 2, CHIPS, rows, width), jnp.bfloat16),
-            dma((8,)), dma((2,)), dma((19,)), dma((2,)), dma((8,)), dma((5,)),
+            dma((5,)), dma((2,)), dma((19,)), dma((2,)), dma((8,)), dma((5,)),
         ],
         compiler_params=pltpu.CompilerParams(
             collective_id=0, has_side_effects=True, vmem_limit_bytes=28 * 2**20

time: 58.7 us -> 58.7 us (level)
  no operation moved by 1% of the time
where the time goes in v8:
time: 58.7 us; the launch traced here: 58.6 us
  Pallas kernels  58 us (99%)
  between operations  0.64 us (1%)
    pallas_call x1, Pallas kernels, gather(): pl.pallas_call(gather_kernel, name='gather', out_shape=(pltpu.VMEM((2, wi...  52 us
    pallas_call x1, Pallas kernels, finish(): pl.pallas_call(finish_kernel, name='finish', out_shape=(jax.ShapeDtypeStr...  5.96 us

profile of v8, /device:TPU:1, one launch (start us, length us, event | category | flops | bytes accessed | tf_op | source)
XLA Modules:
  0.0 58.6 jit_solution(7179156046146752108)
XLA Ops:
  0.6 52.0 %gather.1 = (bf16[2,2048,2048]{2,1,0:T(8,128)(2,1)S(1)}, bf16[16,128]{1,0:T(8,128)(2,1)S(1)}) custom-call(bf16[64,2048]{1,0:T(8,128)(2,1)} %train_gate.1, bf16[16,64]{1,0:T(8,128)(2,1)} %bitcast.3, bf16[16,2048]{1,0:T(8,128)(2,1)} %high_gate.1, bf16[64,2048]{1,0:T(8,128)(2,1)} %train_up.1, bf16[16,64]{1,0:T(8,128)(2,1)} %bitcast.4, ...), custom_call_target="tpu_custom_call" | custom-call | tf_op jit(solution)/shard_map/gather/pallas_call | solution.py:277
  52.6 6.0 %finish.1 = (bf16[2048,2048]{1,0:T(8,128)(2,1)}, bf16[2048,2048]{1,0:T(8,128)(2,1)}, bf16[16,128]{1,0:T(8,128)(2,1)}) custom-call(bf16[2,2048,2048]{2,1,0:T(8,128)(2,1)S(1)} %get-tuple-element.8.turned, bf16[16,128]{1,0:T(8,128)(2,1)S(1)} %get-tuple-element.9.gain), custom_call_target="tpu_custom_call" | custom-call | tf_op jit(solution)/shard_map/finish/pallas_call | solution.py:320

commit v9 on v7

--- a/solution.py
+++ b/solution.py
@@ -122,13 +122,16 @@
         arrive(land.at[:, sibling, pl.ds(0, blocks), :, pl.ds(0, size)], took.at[group])
 
     def turn(chips, ranges=((0, width),)):
-        for k in range(2):
+        def one_array(k, carry):
             for f, s in chips:
-                chip = place(k, f, s)
+                chip = wrap(y + s + k * (f - s)) * SIDE + wrap(x + f + k * (s - f))
                 lanes = pl.ds(pl.multiple_of(chip * LANES, LANES), LANES)
                 for at, size in ranges:
                     tile = [land[k, c, chip, :, pl.ds(at, size)] for c in range(2)]
                     turned[k, pl.ds(at, size), lanes] = jnp.concatenate(tile, axis=0).T
+            return carry
+
+        lax.fori_loop(0, 2, one_array, 0)
 
     def norm_send(pieces, slot):
         for piece, device in pieces:

time: 58.7 us -> 58.8 us (level)
  no operation moved by 1% of the time
where the time goes in v9:
time: 58.8 us; the launch traced here: 58.7 us
  Pallas kernels  58.1 us (99%)
  between operations  0.64 us (1%)
    pallas_call x1, Pallas kernels, gather(): pl.pallas_call(gather_kernel, name='gather', out_shape=(pltpu.VMEM((2, wi...  52.1 us
    pallas_call x1, Pallas kernels, finish(): pl.pallas_call(finish_kernel, name='finish', out_shape=(jax.ShapeDtypeStr...  5.96 us

profile of v9, /device:TPU:1, one launch (start us, length us, event | category | flops | bytes accessed | tf_op | source)
XLA Modules:
  0.0 58.7 jit_solution(18185729887912119022)
XLA Ops:
  0.6 52.1 %gather.1 = (bf16[2,2048,2048]{2,1,0:T(8,128)(2,1)S(1)}, bf16[16,128]{1,0:T(8,128)(2,1)S(1)}) custom-call(bf16[64,2048]{1,0:T(8,128)(2,1)} %train_gate.1, bf16[16,64]{1,0:T(8,128)(2,1)} %bitcast.3, bf16[16,2048]{1,0:T(8,128)(2,1)} %high_gate.1, bf16[64,2048]{1,0:T(8,128)(2,1)} %train_up.1, bf16[16,64]{1,0:T(8,128)(2,1)} %bitcast.4, ...), custom_call_target="tpu_custom_call" | custom-call | tf_op jit(solution)/shard_map/gather/pallas_call | solution.py:274
  52.7 6.0 %finish.1 = (bf16[2048,2048]{1,0:T(8,128)(2,1)}, bf16[2048,2048]{1,0:T(8,128)(2,1)}, bf16[16,128]{1,0:T(8,128)(2,1)}) custom-call(bf16[2,2048,2048]{2,1,0:T(8,128)(2,1)S(1)} %get-tuple-element.8.turned, bf16[16,128]{1,0:T(8,128)(2,1)S(1)} %get-tuple-element.9.gain), custom_call_target="tpu_custom_call" | custom-call | tf_op jit(solution)/shard_map/finish/pallas_call | solution.py:317

commit v10 on v7

--- a/solution.py
+++ b/solution.py
@@ -25,7 +25,7 @@
     y, x, core, col = (lax.axis_index(a) for a in ("y", "x", "core", "cols"))
     sibling = 1 - core
     width = train.shape[2]
-    half, quarter, tail = width // 2, width // 4, width // 8
+    half, quarter, tail = width // 2, width // 4, width // 16
 
     def wrap(i):
         return lax.rem(i + SIDE, SIDE)

time: 58.7 us -> 58.8 us (level)
  no operation moved by 1% of the time
where the time goes in v10:
time: 58.8 us; the launch traced here: 58.7 us
  Pallas kernels  58.1 us (99%)
  between operations  0.64 us (1%)
    pallas_call x1, Pallas kernels, gather(): pl.pallas_call(gather_kernel, name='gather', out_shape=(pltpu.VMEM((2, wi...  52.1 us
    pallas_call x1, Pallas kernels, finish(): pl.pallas_call(finish_kernel, name='finish', out_shape=(jax.ShapeDtypeStr...  5.96 us

profile of v10, /device:TPU:1, one launch (start us, length us, event | category | flops | bytes accessed | tf_op | source)
XLA Modules:
  0.0 58.7 jit_solution(6363211820135092860)
XLA Ops:
  0.6 52.1 %gather.1 = (bf16[2,2048,2048]{2,1,0:T(8,128)(2,1)S(1)}, bf16[16,128]{1,0:T(8,128)(2,1)S(1)}) custom-call(bf16[64,2048]{1,0:T(8,128)(2,1)} %train_gate.1, bf16[16,64]{1,0:T(8,128)(2,1)} %bitcast.3, bf16[16,2048]{1,0:T(8,128)(2,1)} %high_gate.1, bf16[64,2048]{1,0:T(8,128)(2,1)} %train_up.1, bf16[16,64]{1,0:T(8,128)(2,1)} %bitcast.4, ...), custom_call_target="tpu_custom_call" | custom-call | tf_op jit(solution)/shard_map/gather/pallas_call | solution.py:271
  52.7 6.0 %finish.1 = (bf16[2048,2048]{1,0:T(8,128)(2,1)}, bf16[2048,2048]{1,0:T(8,128)(2,1)}, bf16[16,128]{1,0:T(8,128)(2,1)}) custom-call(bf16[2,2048,2048]{2,1,0:T(8,128)(2,1)S(1)} %get-tuple-element.8.turned, bf16[16,128]{1,0:T(8,128)(2,1)S(1)} %get-tuple-element.9.gain), custom_call_target="tpu_custom_call" | custom-call | tf_op jit(solution)/shard_map/finish/pallas_call | solution.py:314
